TPU v7x, 16 devices: a whole 2x2x2 slice. The times are simulated.
16 devices in a mesh: tp: 2 (over z), dp: 8 (over y, x, core).
Axes of the slice: x: 2, y: 2, z: 2, core: 2. Of those that a mesh axis runs over, the one named last changes fastest.
Arguments:
- feats: bfloat16 [1024, 144, 1536], P('dp')
- ln_gamma: float32 [1536], replicated
- ln_beta: float32 [1536], replicated
- w_head: bfloat16 [1536, 22528], P(None, 'tp')
- b_head: float32 [22528], P('tp')
- labels: int32 [1024], P('dp')
Outputs:
- output 1: float32 [], replicated
- output 2: bfloat16 [1024, 144, 1536], P('dp')
- output 3: float32 [1536, 22528], P(None, 'tp')
- output 4: float32 [22528], P('tp')
- output 5: float32 [1536], replicated
- output 6: float32 [1536], replicated
All inputs are finite; a program needn't handle non-finite values.
Results may differ from a plain program's by a relative error of at most 0.001.
Values sent between devices are 32-bit elements.
A program may use at most 1 GiB of HBM per device.

v0:
```python
import jax
import jax.numpy as jnp
from jax import lax
from jax.sharding import PartitionSpec as P

VALID_CLASSES = 21841
LN_EPS = 1e-5
SMOOTH = 0.1


def norm_pool(feats, ln_gamma, ln_beta):
    x_val = feats.astype(jnp.float32)
    mean_x = jnp.mean(x_val, axis=-1, keepdims=True)
    centered = x_val - mean_x
    var_x = jnp.mean(centered * centered, axis=-1, keepdims=True)
    inv_std = lax.rsqrt(var_x + LN_EPS)
    x_hat = centered * inv_std
    x_hat_mean = jnp.mean(x_hat, axis=1)
    pooled16 = (x_hat_mean * ln_gamma + ln_beta).astype(jnp.bfloat16)
    return x_hat, inv_std, x_hat_mean, pooled16


def norm_backward(grad_pool, x_hat, inv_std, x_hat_mean, ln_gamma):
    token_count = x_hat.shape[1]
    grad_gamma = jnp.sum(grad_pool * x_hat_mean, axis=0)
    grad_beta = jnp.sum(grad_pool, axis=0)
    upstream = grad_pool * ln_gamma / token_count
    up_mean = jnp.mean(upstream, axis=-1)
    proj_term = jnp.mean(x_hat * upstream[:, None, :], axis=-1, keepdims=True)
    grad_x = inv_std * (upstream[:, None, :] - up_mean[:, None, None] - x_hat * proj_term)
    return grad_x.astype(jnp.bfloat16), grad_gamma, grad_beta


def solution(mesh):
    data_size = mesh.shape["dp"]

    def local_head(feats, ln_gamma, ln_beta, w_head, b_head, labels):
        shard_cols = w_head.shape[1]
        global_rows = feats.shape[0] * data_size
        x_hat, inv_std, x_hat_mean, pooled16 = norm_pool(feats, ln_gamma, ln_beta)
        col_ids = lax.axis_index("tp") * shard_cols + jnp.arange(shard_cols)
        valid_mask = col_ids < VALID_CLASSES
        logits = jnp.dot(pooled16, w_head, preferred_element_type=jnp.float32) + b_head
        logits = jnp.where(valid_mask, logits, -1e30)
        row_max = lax.pmax(jnp.max(logits, axis=-1), "tp")
        shifted = jnp.exp(logits - row_max[:, None])
        onehot = col_ids == labels[:, None]
        row_stats = jnp.stack([jnp.sum(shifted, axis=-1), jnp.sum(jnp.where(onehot, logits, 0.0), axis=-1), jnp.sum(jnp.where(valid_mask, logits, 0.0), axis=-1)])
        row_stats = lax.psum(row_stats, "tp")
        log_norm = row_max + jnp.log(row_stats[0])
        loss_rows = log_norm - (1.0 - SMOOTH) * row_stats[1] - (SMOOTH / VALID_CLASSES) * row_stats[2]
        soft_probs = shifted / row_stats[0][:, None]
        dlogit = (soft_probs - (1.0 - SMOOTH) * onehot - (SMOOTH / VALID_CLASSES) * valid_mask) / global_rows
        dlogit16 = dlogit.astype(jnp.bfloat16)
        grad_w = lax.psum(lax.dot_general(pooled16, dlogit16, (((0,), (0,)), ((), ())), preferred_element_type=jnp.float32), "dp")
        grad_b = lax.psum(jnp.sum(dlogit, axis=0), "dp")
        grad_pool = lax.dot_general(dlogit16, w_head, (((1,), (1,)), ((), ())), preferred_element_type=jnp.float32)
        grad_pool = lax.psum(grad_pool, "tp")
        grad_feats, grad_gamma, grad_beta = norm_backward(grad_pool, x_hat, inv_std, x_hat_mean, ln_gamma)
        loss_sum, grad_gamma, grad_beta = lax.psum((jnp.sum(loss_rows), grad_gamma, grad_beta), "dp")
        return loss_sum / global_rows, grad_feats, grad_w, grad_b, grad_gamma, grad_beta

    return jax.shard_map(local_head, mesh=mesh, in_specs=(P("dp", None, None), P(), P(), P(None, "tp"), P("tp"), P("dp")), out_specs=(P(), P("dp", None, None), P(None, "tp"), P("tp"), P(), P()), check_vma=False)
```

profile of v0, /device:TPU:0, one launch (start us, length us, event | category | flops | bytes accessed | tf_op | source)
XLA Modules:
  0.0 1041.2 jit_solution(10341412998126452186)
XLA Ops:
  7.2 0.0 all-reduce.4.cloned.1.call-start
  7.3 22.6 %convert_reduce_fusion = f32[128,144]{1,0:T(8,128)S(1)} fusion(bf16[128,144,1536]{2,1,0:T(8,128)(2,1)} %param.6), kind=kLoop, calls=%fused_computation.1 | loop fusion | flops 56604672 | bytes 56696832 | tf_op jit(solution)/shard_map/reduce_sum | solution.py:13
  29.9 23.6 %fusion.9 = f32[128,144]{1,0:T(8,128)S(1)} fusion(bf16[128,144,1536]{2,1,0:T(8,128)(2,1)} %param.6, f32[128,144]{1,0:T(8,128)S(1)} %broadcast_multiply_fusion.1), kind=kLoop, calls=%fused_computation.11 | loop fusion | flops 113227776 | bytes 56770560 | tf_op jit(solution)/shard_map/reduce_sum | solution.py:15
  53.5 0.0 copy-start.2
  53.6 69.9 %fusion.4 = f32[128,1536]{1,0:T(8,128)S(1)} fusion(bf16[128,144,1536]{2,1,0:T(8,128)(2,1)} %param.6, f32[128,144]{1,0:T(8,128)S(1)} %add_rsqrt_fusion, f32[128,144]{1,0:T(8,128)S(1)} %broadcast_multiply_fusion.1), kind=kLoop, calls=%fused_computation.6 | loop fusion | flops 113049600 | bytes 57556992 | tf_op jit(solution)/shard_map/reduce_sum | solution.py:18
  123.5 18.4 %fusion.26 = (f32[128]{0:T(128)S(1)}, f32[128,11264]{1,0:T(8,128)}) fusion(f32[11264]{0:T(1024)S(1)} %copy-done.1, bf16[1536,11264]{1,0:T(8,128)(2,1)} %param.9, f32[128,1536]{1,0:T(8,128)S(1)} %fusion.4, f32[1536]{0:T(1024)S(1)} %copy-done, f32[1536]{0:T(1024)S(1)} %broadcast_multiply_fusion.2, pred[11264]{0:T(1024)(128)(4,1)S(1)} %broadcast_compare_fusion), kind=kOutput, calls=%fused_computation.47 | convolution fusion | flops 4434100224 | bytes 41225728 | tf_op jit(solution)/shard_map/dot_general | solution.py:43
  141.9 6.2 pmax.7
  148.1 4.2 fusion.15
  152.3 5.1 psum.49
  157.4 18.7 %fusion.18 = f32[128,1536]{1,0:T(8,128)} fusion(bf16[1536,11264]{1,0:T(8,128)(2,1)} %param.9, f32[128,11264]{1,0:T(8,128)} %get-tuple-element.20, f32[11264]{0:T(1024)S(1)} %broadcast_select_fusion, f32[128]{0:T(128)S(1)} %slice_bitcast_fusion, s32[11264]{0:T(1024)S(1)} %iota_add_fusion, f32[128]{0:T(128)S(1)} %pmax.7, s32[128]{0:T(128)S(1)} %copy-done.3), kind=kOutput, calls=%fused_computation.25 | convolution fusion | flops 4440719360 | bytes 41248256 | tf_op jit(solution)/shard_map/dot_general | solution.py:57
  176.1 0.0 all-reduce.4.cloned.1.call-update
  176.2 0.0 all-reduce.6.cloned.1.call-start
  176.2 28.8 %fusion.16 = f32[1536,11264]{1,0:T(8,128)} fusion(f32[128,1536]{1,0:T(8,128)S(1)} %fusion.4, f32[1536]{0:T(1024)S(1)} %copy-done, f32[1536]{0:T(1024)S(1)} %broadcast_multiply_fusion.2, f32[128,11264]{1,0:T(8,128)} %get-tuple-element.20, f32[11264]{0:T(1024)S(1)} %broadcast_select_fusion, f32[128]{0:T(128)S(1)} %slice_bitcast_fusion, ...), kind=kOutput, calls=%fused_computation.23 | convolution fusion | flops 4441309184 | bytes 75863552 | tf_op jit(solution)/shard_map/dot_general | solution.py:55
  205.0 0.0 all-reduce.6.cloned.1.call-update
  205.0 0.6 fusion.20
  205.7 4.0 fusion.22
  209.7 0.0 all-reduce.4.cloned.1.call-done
  209.7 1.4 fusion.25
  211.1 24.6 %all-reduce = (f32[]{:T(128)}, f32[11264]{0:T(1024)}, f32[1536]{0:T(1024)}, f32[1536]{0:T(1024)}) all-reduce(f32[]{:T(128)} %fusion.20, f32[11264]{0:T(1024)S(1)} %fusion.22, f32[1536]{0:T(1024)S(1)} %get-tuple-element.17, f32[1536]{0:T(1024)S(1)} %get-tuple-element.18), channel_id=1, replica_groups=mesh['tp'=2,'dp'=8] {'dp'}, use_global_device_ids=true, to_apply=%region_10.11 | all-reduce | flops 14337 | bytes 114696 | tf_op jit(solution)/shard_map/psum | solution.py:60
  236.4 27.7 %fusion.5 = f32[128,144]{1,0:T(8,128)S(1)} fusion(bf16[128,144,1536]{2,1,0:T(8,128)(2,1)} %param.6, f32[128,1536]{1,0:T(8,128)S(1)} %get-tuple-element.16, f32[128,144]{1,0:T(8,128)S(1)} %add_rsqrt_fusion, f32[128,144]{1,0:T(8,128)S(1)} %broadcast_multiply_fusion.1), kind=kLoop, calls=%fused_computation.7 | loop fusion | flops 141539328 | bytes 57630720 | tf_op jit(solution)/shard_map/reduce_sum | solution.py:29
  264.1 0.1 broadcast_subtract_fusion
  264.3 37.6 %fusion.8 = bf16[128,144,1536]{2,1,0:T(8,128)(2,1)} fusion(bf16[128,144,1536]{2,1,0:T(8,128)(2,1)} %param.6, f32[128,144]{1,0:T(8,128)S(1)} %broadcast_multiply_fusion, f32[128,1536]{1,0:T(8,128)S(1)} %broadcast_subtract_fusion, f32[128,144]{1,0:T(8,128)S(1)} %add_rsqrt_fusion, f32[128,144]{1,0:T(8,128)S(1)} %broadcast_multiply_fusion.1), kind=kLoop, calls=%fused_computation.10 | loop fusion | flops 198180864 | bytes 114253824 | tf_op jit(solution)/shard_map/convert_element_type | solution.py:31
  301.9 687.1 %all-reduce.6.cloned.1.call-done = f32[1536,11264]{1,0:T(8,128)} async-done(((f32[1536,11264]{1,0:T(8,128)}), f32[1536,11264]{1,0:T(8,128)}) %all-reduce.6.cloned.1.call-update) | async-done | bytes 69206032 | tf_op jit(solution)/shard_map/psum | solution.py:55
  988.9 44.3 %copy.14 = f32[1536,11264]{1,0:T(8,128)} copy(f32[1536,11264]{1,0:T(8,128)} %all-reduce.6.cloned.1.call-done) | data formatting | bytes 138412032
  (17 shorter events, 0.1 us)
Async XLA Ops:
  7.2 202.5 %all-reduce.4.cloned.1.call-start = ((), (), s32[]{:S(2)}) async-start(), calls=%async_computation | async-start | bytes 1572864 | tf_op jit(solution)/shard_map/psum | solution.py:58
  53.5 70.0 %copy-start.2 = (f32[1536]{0:T(1024)S(1)}, f32[1536]{0:T(1024)}, u32[]{:S(2)}) copy-start(f32[1536]{0:T(1024)} %param.7) | copy-start | bytes 18436
  53.5 70.0 %copy-start = (f32[1536]{0:T(1024)S(1)}, f32[1536]{0:T(1024)}, u32[]{:S(2)}) copy-start(f32[1536]{0:T(1024)} %param.8) | copy-start | bytes 18436
  53.6 70.0 %copy-start.1 = (f32[11264]{0:T(1024)S(1)}, f32[11264]{0:T(1024)}, u32[]{:S(2)}) copy-start(f32[11264]{0:T(1024)} %param.10) | copy-start | bytes 135172
  123.5 24.6 %copy-start.3 = (s32[128]{0:T(128)S(1)}, s32[128]{0:T(128)}, u32[]{:S(2)}) copy-start(s32[128]{0:T(128)} %param.11) | copy-start | bytes 1540
  176.2 812.8 %all-reduce.6.cloned.1.call-start = ((), (), s32[]{:S(2)}) async-start(), calls=%async_computation.1 | async-start | bytes 138412032 | tf_op jit(solution)/shard_map/psum | solution.py:55
Sparse Core Ops, SparseCore 0:
  176.3 31.9 all-reduce.3
  212.6 776.2 all-reduce.5
where the time goes:
time: 1040 us
  waiting for transfers between devices  687 us (66%)
  other arithmetic  192 us (18%)
  matrix products  65.9 us (6%)
  local copies, waits for them, and re-layouts  44.4 us (4%)
  blocking collectives  36 us (3%)
  between operations  16 us (2%)
    psum x1, waiting for transfers between devices, local_head(): lax.psum(lax.dot_general(pooled16, dlogit16, (((0,), (0,)), ((), ())), pr...  687 us
    reduce_sum x1, other arithmetic, norm_pool(): x_hat_mean = jnp.mean(x_hat, axis=1)  69.9 us
    unnamed x9, local copies, waits for them, and re-layouts  44.4 us
    convert_element_type x1, other arithmetic, norm_backward(): return (grad_x.astype(jnp.bfloat16), grad_gamma, grad_beta)  37.6 us
    dot_general x1, matrix products, local_head(): lax.dot_general(pooled16, dlogit16, (((0,), (0,)), ((), ())), preferred_e...  28.8 us
    reduce_sum x1, other arithmetic, norm_backward(): proj_term = jnp.mean(x_hat * upstream[:, None, :], axis=-1, keepdims=True)  27.7 us
    psum x1, blocking collectives, local_head(): lax.psum((jnp.sum(loss_rows), grad_gamma, grad_beta), 'dp')  24.6 us
    reduce_sum x1, other arithmetic, norm_pool(): var_x = jnp.mean(centered * centered, axis=-1, keepdims=True)  23.6 us
  transfers between devices with their start and end apart: 2, of which 1 were waited for; matrix products, arithmetic and copies ran while one was open for 10% of the time, Pallas kernels for 0%

commit v1 on v0

v1 whole, which is shorter than its diff:
```python
import functools
import math

import jax
import jax.numpy as jnp
from jax import lax
from jax.experimental import pallas as pl
from jax.experimental.pallas import tpu as pltpu
from jax.sharding import PartitionSpec as P

VALID_CLASSES = 21841
LN_EPS = 1e-5
SMOOTH = 0.1
LANES = 128
COLS = 512
SUB = 256
IMGS = 8
ROW_TILE = 16


def norm_kernel(x_ref, pool_ref, mean_ref, inv_ref):
    imgs, tokens, width = x_ref.shape
    chunks = tokens // ROW_TILE
    lane = lax.broadcasted_iota(jnp.int32, (ROW_TILE, LANES), 1)

    def one_image(i, carry):
        means, invs = [], []
        for c in range(chunks):
            x = x_ref[i, pl.ds(c * ROW_TILE, ROW_TILE), :].astype(jnp.float32)
            means.append(jnp.sum(x, axis=1, keepdims=True) * (1.0 / width))
        for c in range(chunks):
            x = x_ref[i, pl.ds(c * ROW_TILE, ROW_TILE), :].astype(jnp.float32) - means[c]
            var = jnp.sum(x * x, axis=1, keepdims=True) * (1.0 / width)
            invs.append(lax.rsqrt(var + LN_EPS))
        total = jnp.zeros((ROW_TILE, width), jnp.float32)
        for c in range(chunks):
            x = x_ref[i, pl.ds(c * ROW_TILE, ROW_TILE), :].astype(jnp.float32) - means[c]
            total = total + x * invs[c]
            rows = pl.ds(c * ROW_TILE, ROW_TILE)
            mean_ref[0, rows, :] = jnp.where(lane == i, means[c], mean_ref[0, rows, :])
            inv_ref[0, rows, :] = jnp.where(lane == i, invs[c], inv_ref[0, rows, :])
        pool_ref[pl.ds(i, 1), :] = jnp.sum(total, axis=0, keepdims=True) * (1.0 / tokens)
        return carry

    lax.fori_loop(0, imgs, one_image, 0)


def norm_call(feats):
    rows, tokens, width = feats.shape
    stat = jax.ShapeDtypeStruct((rows // IMGS, tokens, LANES), jnp.float32)
    return pl.pallas_call(
        norm_kernel,
        name="norm_pool",
        grid=(rows // IMGS,),
        in_specs=[pl.BlockSpec((IMGS, tokens, width), lambda g: (g, 0, 0))],
        out_specs=[
            pl.BlockSpec((IMGS, width), lambda g: (g, 0)),
            pl.BlockSpec((1, tokens, LANES), lambda g: (g, 0, 0)),
            pl.BlockSpec((1, tokens, LANES), lambda g: (g, 0, 0)),
        ],
        out_shape=[jax.ShapeDtypeStruct((rows, width), jnp.float32), stat, stat],
        compiler_params=pltpu.CompilerParams(vmem_limit_bytes=48 * 2**20),
        cost_estimate=pl.CostEstimate(flops=10 * rows * tokens * width, bytes_accessed=2 * rows * tokens * width, transcendentals=0),
    )(feats)


def wide(column_tile):
    return jnp.concatenate([column_tile] * (SUB // LANES), axis=1)


def head_block(shard_cols, block, rows_total, p_ref, pt_ref, lse_ref, y_ref, w_ref, b_ref, dw_ref, db_ref, dl_ref):
    rows = p_ref.shape[0]
    base = lax.axis_index("tp") * shard_cols + block * COLS
    for s in range(COLS // SUB):
        sub = pl.ds(s * SUB, SUB)
        logits = jnp.dot(p_ref[...], w_ref[:, sub], preferred_element_type=jnp.float32)
        col = base + s * SUB + lax.broadcasted_iota(jnp.int32, (1, SUB), 1)
        valid = col < VALID_CLASSES
        smooth = jnp.where(valid, SMOOTH / VALID_CLASSES, 0.0)
        target = smooth + (1.0 - SMOOTH)
        bias = jnp.where(valid, b_ref[:, sub], -jnp.inf)
        soft = jnp.exp((logits + bias) - wide(lse_ref[...]))
        dlogit = (soft - jnp.where(wide(y_ref[...]) == col, target, smooth)) * (1.0 / rows_total)
        db_ref[:, sub] = jnp.sum(dlogit, axis=0, keepdims=True)
        dl_ref[s] = dlogit.astype(jnp.bfloat16)
    for s in range(COLS // SUB):
        dw_ref[:, pl.ds(s * SUB, SUB)] = jnp.dot(pt_ref[...], dl_ref[s], preferred_element_type=jnp.float32)


def head_kernel(shard_cols, rows_total, p_ref, pt_ref, lse_ref, y_ref, w_ref, b_ref, dw_ref, db_ref, dl_ref):
    head_block(shard_cols, pl.program_id(0), rows_total, p_ref, pt_ref, lse_ref, y_ref, w_ref, b_ref, dw_ref, db_ref, dl_ref)


def head_feat_kernel(shard_cols, rows_total, first, p_ref, pt_ref, lse_ref, y_ref, w_ref, b_ref, x_ref, mean_ref, inv_ref, u_ref, um_ref, dw_in, db_in, dw_ref, db_ref, df_ref, dl_ref):
    imgs, tokens, width = x_ref.shape
    chunks = tokens // ROW_TILE
    for i in range(imgs):
        u = u_ref[pl.ds(i, 1), :]
        um = um_ref[pl.ds(i, 1), :][:, :1]
        for c in range(chunks):
            rows = pl.ds(c * ROW_TILE, ROW_TILE)
            mean = mean_ref[0, rows, pl.ds(i, 1)]
            inv = inv_ref[0, rows, pl.ds(i, 1)]
            x = x_ref[i, rows, :].astype(jnp.float32)
            proj = jnp.sum((x - mean) * u, axis=1, keepdims=True) * (inv * (1.0 / width))
            slope = -(inv * inv * proj)
            offset = -(inv * um) - slope * mean
            x = x_ref[i, rows, :].astype(jnp.float32)
            df_ref[i, rows, :] = (x * slope + (u * inv + offset)).astype(jnp.bfloat16)
    head_block(shard_cols, pl.program_id(0) + first, rows_total, p_ref, pt_ref, lse_ref, y_ref, w_ref, b_ref, dw_ref, db_ref, dl_ref)


def resident(shape):
    return pl.BlockSpec(shape, lambda g: (0,) * len(shape), pipeline_mode=pl.Buffered(1))


def head_specs(rows, width, first):
    return [
        resident((rows, width)),
        resident((width, rows)),
        resident((rows, LANES)),
        resident((rows, LANES)),
        pl.BlockSpec((width, COLS), lambda g: (0, g + first)),
        pl.BlockSpec((1, COLS), lambda g: (0, g + first)),
    ]


def head_calls(p_all, lse_all, y_all, w_head, b_head, feats, mean, inv, make_u):
    rows, width = p_all.shape
    shard_cols = w_head.shape[1]
    imgs_all, tokens, _ = feats.shape
    steps = shard_cols // COLS
    feat_steps = imgs_all // IMGS
    first = steps - feat_steps
    pt_all = p_all.T
    lse_b = jnp.broadcast_to(lse_all[:, None], (rows, LANES))
    y_b = jnp.broadcast_to(y_all[:, None], (rows, LANES))
    b_row = b_head[None, :]
    head_args = (p_all, pt_all, lse_b, y_b, w_head, b_row)
    dw_shape = jax.ShapeDtypeStruct((width, shard_cols), jnp.float32)
    db_shape = jax.ShapeDtypeStruct((1, shard_cols), jnp.float32)
    params = pltpu.CompilerParams(vmem_limit_bytes=60 * 2**20)
    scratch = [pltpu.VMEM((COLS // SUB, rows, SUB), jnp.bfloat16)]

    def cost(n):
        return pl.CostEstimate(flops=4 * rows * width * COLS * n, bytes_accessed=6 * width * COLS * n, transcendentals=rows * COLS * n)

    dw, db = pl.pallas_call(
        functools.partial(head_kernel, shard_cols, rows),
        name="head_first",
        grid=(first,),
        in_specs=head_specs(rows, width, 0),
        out_specs=[pl.BlockSpec((width, COLS), lambda g: (0, g)), pl.BlockSpec((1, COLS), lambda g: (0, g))],
        out_shape=[dw_shape, db_shape],
        scratch_shapes=scratch,
        compiler_params=params,
        cost_estimate=cost(first),
    )(*head_args)
    u, um = make_u()
    um_b = jnp.broadcast_to(um[:, None], (imgs_all, LANES))
    img = lambda shape: pl.BlockSpec(shape, lambda g: (g,) + (0,) * (len(shape) - 1))
    n_in = 11
    dw, db, df = pl.pallas_call(
        functools.partial(head_feat_kernel, shard_cols, rows, first),
        name="head_rest",
        grid=(feat_steps,),
        in_specs=head_specs(rows, width, first)
        + [img((IMGS, tokens, width)), img((1, tokens, LANES)), img((1, tokens, LANES)), img((IMGS, width)), img((IMGS, LANES))]
        + [pl.BlockSpec(memory_space=pl.ANY)] * 2,
        out_specs=[
            pl.BlockSpec((width, COLS), lambda g: (0, g + first)),
            pl.BlockSpec((1, COLS), lambda g: (0, g + first)),
            img((IMGS, tokens, width)),
        ],
        out_shape=[dw_shape, db_shape, jax.ShapeDtypeStruct(feats.shape, jnp.bfloat16)],
        scratch_shapes=scratch,
        input_output_aliases={n_in: 0, n_in + 1: 1},
        compiler_params=params,
        cost_estimate=cost(feat_steps),
    )(*head_args, feats, mean, inv, u, um_b, dw, db)
    return dw, db[0], df


def solution(mesh):
    def local_head(feats, ln_gamma, ln_beta, w_head, b_head, labels):
        shard_cols = w_head.shape[1]
        tokens = feats.shape[1]
        xhat_mean, mean, inv = norm_call(feats)
        pool_all = lax.all_gather(xhat_mean, "dp", axis=0, tiled=True)
        p_all = (pool_all * ln_gamma + ln_beta).astype(jnp.bfloat16)
        y_all = lax.all_gather(labels, "dp", axis=0, tiled=True)
        rows = p_all.shape[0]

        pooled16 = (xhat_mean * ln_gamma + ln_beta).astype(jnp.bfloat16)
        col_ids = lax.axis_index("tp") * shard_cols + jnp.arange(shard_cols)
        valid = col_ids < VALID_CLASSES
        logits = jnp.dot(pooled16, w_head, preferred_element_type=jnp.float32) + b_head
        logits = jnp.where(valid, logits, -1e30)
        row_max = lax.pmax(jnp.max(logits, axis=-1), "tp")
        shifted = jnp.exp(logits - row_max[:, None])
        onehot = col_ids == labels[:, None]
        stats = jnp.stack([jnp.sum(shifted, axis=-1), jnp.sum(jnp.where(onehot, logits, 0.0), axis=-1), jnp.sum(jnp.where(valid, logits, 0.0), axis=-1)])
        stats = lax.psum(stats, "tp")
        lse = row_max + jnp.log(stats[0])
        loss_rows = lse - (1.0 - SMOOTH) * stats[1] - (SMOOTH / VALID_CLASSES) * stats[2]
        lse_all = lax.all_gather(lse, "dp", axis=0, tiled=True)
        soft = shifted / stats[0][:, None]
        dlogit16 = ((soft - (1.0 - SMOOTH) * onehot - (SMOOTH / VALID_CLASSES) * valid) / rows).astype(jnp.bfloat16)
        dpool_part = lax.dot_general(dlogit16, w_head, (((1,), (1,)), ((), ())), preferred_element_type=jnp.float32)
        dpool_other = lax.ppermute(dpool_part, "tp", [(0, 1), (1, 0)])
        small = (jnp.sum(loss_rows), jnp.sum(dpool_part * xhat_mean, axis=0), jnp.sum(dpool_part, axis=0))

        def make_u():
            u = (dpool_part + dpool_other) * ln_gamma / tokens
            return u, jnp.mean(u, axis=-1)

        dw, db, df = head_calls(p_all, lse_all, y_all, w_head, b_head, feats, mean, inv, make_u)
        loss_sum = lax.psum(small[0], "dp")
        dgamma, dbeta = lax.psum((small[1], small[2]), ("dp", "tp"))
        return loss_sum / rows, df, dw, db, dgamma, dbeta

    return jax.shard_map(local_head, mesh=mesh, in_specs=(P("dp", None, None), P(), P(), P(None, "tp"), P("tp"), P("dp")), out_specs=(P(), P("dp", None, None), P(None, "tp"), P("tp"), P(), P()), check_vma=False)
```

time: 1040 us -> 438 us (0.42)
  waiting for transfers between devices: 687 us -> 0.03 us
  Pallas kernels: 0 us -> 285 us
  other arithmetic: 192 us -> 14.9 us
  blocking collectives: 36 us -> 72.4 us
  local copies, waits for them, and re-layouts: 44.4 us -> 10.7 us
  matrix products: 65.9 us -> 36.6 us
    psum x2 -> x0, waiting for transfers between devices: 687 us -> none  [the longest x1 687 us: local_head(): lax.psum(lax.dot_general(pooled16, dlogit16, (((0,), (0,)), ((), ())), pr...]
    pallas_call x0 -> x3, Pallas kernels: none -> 285 us  [the longest x1 202 us: head_calls(): pl.pallas_call(functools.partial(head_feat_kernel, shard_cols, rows, firs...]
    reduce_sum x7 -> x1, other arithmetic: 150 us -> 1.15 us  [local_head(): jnp.sum(dpool_part, axis=0)]
    unnamed x9 -> x12, local copies, waits for them, and re-layouts: 44.4 us -> 2.11 us
    convert_element_type x1, other arithmetic: 37.6 us -> 4.49 us  [local_head(): p_all = (pool_all * ln_gamma + ln_beta).astype(jnp.bfloat16)]
    dot_general x1 -> x0, matrix products: 28.8 us -> none  [local_head(): lax.dot_general(pooled16, dlogit16, (((0,), (0,)), ((), ())), preferred_e...]
    psum x2 -> x3, blocking collectives: 29.8 us -> 49.6 us  [the longest x1 32.2 us: local_head(): dgamma, dbeta = lax.psum((small[1], small[2]), ('dp', 'tp'))]
    all_gather x0 -> x2, blocking collectives: none -> 16.6 us  [the longest x1 8.83 us: local_head(): y_all = lax.all_gather(labels, 'dp', axis=0, tiled=True)]
  transfers between devices with their start and end apart: 2 -> 2, of which waited for: 1 -> 0; matrix products, arithmetic and copies ran while one was open for 10% -> 10% of each run, Pallas kernels for 0% -> 0%
where the time goes in v1:
time: 438 us; the launch traced here: 437 us
  Pallas kernels  285 us (65%)
  blocking collectives  72.4 us (17%)
  matrix products  36.6 us (8%)
  between operations  15.9 us (4%)
  other arithmetic  14.9 us (3%)
  local copies, waits for them, and re-layouts  10.7 us (2%)
    pallas_call x1, Pallas kernels, head_calls(): pl.pallas_call(functools.partial(head_feat_kernel, shard_cols, rows, firs...  202 us
    pallas_call x1, Pallas kernels, norm_call(): pl.pallas_call(norm_kernel, name='norm_pool', grid=(rows // IMGS,), in_sp...  54.8 us
    psum x1, blocking collectives, local_head(): dgamma, dbeta = lax.psum((small[1], small[2]), ('dp', 'tp'))  32.2 us
    pallas_call x1, Pallas kernels, head_calls(): pl.pallas_call(functools.partial(head_kernel, shard_cols, rows), name='he...  27.6 us
    dot_general x1, matrix products, local_head(): jnp.dot(pooled16, w_head, preferred_element_type=jnp.float32) + b_head  18.4 us
    dot_general x1, matrix products, local_head(): lax.dot_general(dlogit16, w_head, (((1,), (1,)), ((), ())), preferred_ele...  18.3 us
    psum x1, blocking collectives, local_head(): loss_sum = lax.psum(small[0], 'dp')  12.4 us
    all_gather x1, blocking collectives, local_head(): y_all = lax.all_gather(labels, 'dp', axis=0, tiled=True)  8.83 us
  transfers between devices with their start and end apart: 2, of which 0 were waited for; matrix products, arithmetic and copies ran while one was open for 10% of the time, Pallas kernels for 0%

profile of v1, /device:TPU:0, one launch (start us, length us, event | category | flops | bytes accessed | tf_op | source)
XLA Modules:
  0.0 437.4 jit_solution(5700803970229307033)
XLA Ops:
  7.2 54.8 %norm_pool.1 = (f32[128,1536]{1,0:T(8,128)S(1)}, f32[16,144,128]{2,1,0:T(8,128)S(1)}, f32[16,144,128]{2,1,0:T(8,128)S(1)}) custom-call(bf16[128,144,1536]{2,1,0:T(8,128)(2,1)} %x_ref.3), custom_call_target="tpu_custom_call" | custom-call | flops 283115520 | bytes 56623104 | tf_op jit(solution)/shard_map/norm_pool/pallas_call | solution.py:51
  62.0 1.1 copy-done
  63.1 1.0 copy-done.1
  64.1 1.1 copy.17
  65.4 18.4 %fusion.26 = (f32[128]{0:T(128)S(1)}, f32[128,11264]{1,0:T(8,128)}) fusion(f32[11264]{0:T(1024)S(1)} %copy-done.4, bf16[1536,11264]{1,0:T(8,128)(2,1)} %w_ref.3, f32[128,1536]{1,0:T(8,128)S(1)} %get-tuple-element.14, f32[1536]{0:T(1024)S(1)} %copy-done.3, f32[1536]{0:T(1024)S(1)} %copy-done.2, pred[11264]{0:T(1024)(128)(4,1)S(1)} %broadcast_compare_fusion), kind=kOutput, calls=%fused_computation.43 | convolution fusion | flops 4434100224 | bytes 41225728 | tf_op jit(solution)/shard_map/dot_general | solution.py:197
  83.7 6.2 %pmax.7 = f32[128]{0:T(128)S(1)} all-reduce(f32[128]{0:T(128)S(1)} %get-tuple-element.35), channel_id=1, replica_groups=mesh['tp'=2,'dp'=8] {'tp'}, use_global_device_ids=true, to_apply=%region_1.2 | all-reduce | flops 128 | bytes 1024 | tf_op jit(solution)/shard_map/pmax | solution.py:199
  89.9 4.2 fusion.6
  94.1 4.9 %psum.28 = f32[3,128]{1,0:T(4,128)S(1)} all-reduce(f32[3,128]{1,0:T(4,128)S(1)} %pad_maximum_fusion), channel_id=1, replica_groups=mesh['tp'=2,'dp'=8] {'tp'}, use_global_device_ids=true, to_apply=%region_5.6 | all-reduce | flops 384 | bytes 3072 | tf_op jit(solution)/shard_map/psum | solution.py:203
  99.1 18.3 %fusion.7 = f32[128,1536]{1,0:T(8,128)S(1)} fusion(bf16[1536,11264]{1,0:T(8,128)(2,1)} %w_ref.3, f32[128,11264]{1,0:T(8,128)} %get-tuple-element.36, f32[11264]{0:T(1024)S(1)} %broadcast_select_fusion, f32[128]{0:T(128)S(1)} %slice_bitcast_fusion, s32[11264]{0:T(1024)S(1)} %iota_add_fusion, f32[128]{0:T(128)S(1)} %pmax.7, s32[128]{0:T(128)S(1)} %copy-done.5), kind=kOutput, calls=%fused_computation.13 | convolution fusion | flops 4440719360 | bytes 41248256 | tf_op jit(solution)/shard_map/dot_general | solution.py:209
  117.4 2.1 collective-permute-start
  119.4 0.6 fusion.23
  120.0 12.4 %psum.29 = f32[]{:T(128)} all-reduce(f32[]{:T(128)} %get-tuple-element.34), channel_id=1, replica_groups=mesh['tp'=2,'dp'=8] {'dp'}, use_global_device_ids=true, to_apply=%region_7.8 | all-reduce | flops 1 | bytes 8 | tf_op jit(solution)/shard_map/psum | solution.py:218
  133.1 8.8 %all-gather.1 = s32[8,1,128]{2,1,0:T(1,128)S(1)} all-gather(s32[1,1,128]{2,1,0:T(1,128)S(1)} %bitcast.32), channel_id=1, replica_groups=mesh['tp'=2,'dp'=8] {'dp'}, dimensions={0}, use_global_device_ids=true | all-gather | bytes 4608 | tf_op jit(solution)/shard_map/all_gather | solution.py:191
  141.9 7.8 %all-gather = f32[8,1,128]{2,1,0:T(1,128)S(1)} all-gather(f32[1,1,128]{2,1,0:T(1,128)S(1)} %get-tuple-element.33), channel_id=1, replica_groups=mesh['tp'=2,'dp'=8] {'dp'}, dimensions={0}, use_global_device_ids=true | all-gather | bytes 4608 | tf_op jit(solution)/shard_map/all_gather | solution.py:206
  149.7 1.1 fusion.24
  150.9 32.2 %all-reduce = (f32[1536]{0:T(1024)}, f32[1536]{0:T(1024)}) all-reduce(f32[1536]{0:T(1024)S(1)} %get-tuple-element.26, f32[1536]{0:T(1024)S(1)} %get-tuple-element.25), channel_id=1, replica_groups=mesh['tp'=2,'dp'=8] {'dp','tp'}, use_global_device_ids=true, to_apply=%region_10.11 | all-reduce | flops 3072 | bytes 24576 | tf_op jit(solution)/shard_map/psum | solution.py:219
  183.1 4.5 %add_convert_fusion = bf16[1024,1536]{0,1:T(8,128)(2,1)} fusion(f32[1024,1536]{0,1:T(8,128)} %all-gather.4.cloned.1.call-done, f32[1536]{0:T(1024)S(1)} %copy-done.3, f32[1536]{0:T(1024)S(1)} %copy-done.2), kind=kLoop, calls=%fused_computation.4 | loop fusion | flops 4718592 | bytes 9449472 | tf_op jit(solution)/shard_map/convert_element_type | solution.py:190
  187.6 4.7 %copy.19.p_ref = bf16[1024,1536]{1,0:T(8,128)(2,1)} copy(bf16[1024,1536]{0,1:T(8,128)(2,1)} %add_convert_fusion) | data formatting | bytes 6291456 | tf_op jit(solution)/shard_map/convert_element_type | solution.py:190
  192.3 4.5 %fusion.29.pt_ref = bf16[1536,1024]{1,0:T(8,128)(2,1)} fusion(f32[1536]{0:T(1024)S(1)} %copy-done.3, f32[1024,1536]{0,1:T(8,128)} %all-gather.4.cloned.1.call-done, f32[1536]{0:T(1024)S(1)} %copy-done.2), kind=kLoop, calls=%fused_computation.44 | loop fusion | flops 4718592 | bytes 9449472 | tf_op jit(solution)/shard_map/transpose | solution.py:135
  196.8 1.0 broadcast_in_dim.26.y_ref
  197.8 1.0 broadcast_in_dim.25.lse_ref
  198.8 27.6 %head_first.1 = (f32[1536,11264]{1,0:T(8,128)}, f32[1,11264]{1,0:T(1,128)}) custom-call(bf16[1024,1536]{1,0:T(8,128)(2,1)} %copy.19.p_ref, bf16[1536,1024]{1,0:T(8,128)(2,1)} %fusion.29.pt_ref, f32[1024,128]{1,0:T(8,128)} %broadcast_in_dim.25.lse_ref, s32[1024,128]{1,0:T(8,128)} %broadcast_in_dim.26.y_ref, bf16[1536,11264]{1,0:T(8,128)(2,1)} %w_ref.3, ...), custom_call_target="tpu_custom_call" | custom-call | flops 19327352832 | bytes 28311552 | tf_op jit(solution)/shard_map/head_first/pallas_call | solution.py:148
  226.4 0.7 broadcast_in_dim.28.um_ref
  227.1 202.3 %head_rest.1 = (f32[1536,11264]{1,0:T(8,128)}, f32[1,11264]{1,0:T(1,128)}, bf16[128,144,1536]{2,1,0:T(8,128)(2,1)}) custom-call(bf16[1024,1536]{1,0:T(8,128)(2,1)} %copy.19.p_ref, bf16[1536,1024]{1,0:T(8,128)(2,1)} %fusion.29.pt_ref, f32[1024,128]{1,0:T(8,128)} %broadcast_in_dim.25.lse_ref, ...), custom_call_target="tpu_custom_call", output_to_operand_aliasing={{0}: (11, {}), {1}: (12, {})} | custom-call | flops 51539607552 | bytes 75497472 | tf_op jit(solution)/shard_map/head_rest/pallas_call | solution.py:163
  (20 shorter events, 0.1 us)
Async XLA Ops:
  7.2 58.2 %copy-start.2 = (f32[1536]{0:T(1024)S(1)}, f32[1536]{0:T(1024)}, u32[]{:S(2)}) copy-start(f32[1536]{0:T(1024)} %param.7) | copy-start | bytes 18436
  7.2 58.2 %copy-start.3 = (f32[1536]{0:T(1024)S(1)}, f32[1536]{0:T(1024)}, u32[]{:S(2)}) copy-start(f32[1536]{0:T(1024)} %param.8) | copy-start | bytes 18436
  7.2 58.2 %copy-start.4 = (f32[11264]{0:T(1024)S(1)}, f32[11264]{0:T(1024)}, u32[]{:S(2)}) copy-start(f32[11264]{0:T(1024)} %param.10) | copy-start | bytes 135172
  7.2 175.9 %all-gather.4.cloned.1.call-start = ((), (), s32[]{:S(2)}) async-start(), calls=%async_computation | async-start | bytes 7077888 | tf_op jit(solution)/shard_map/all_gather | solution.py:189
  62.0 1.1 copy-start
  63.1 1.0 copy-start.1
  65.4 24.6 %copy-start.5 = (s32[128]{0:T(128)S(1)}, s32[128]{0:T(128)}, u32[]{:S(2)}) copy-start(s32[128]{0:T(128)} %param.11) | copy-start | bytes 1540
  117.4 32.4 %collective-permute-start = (f32[128,1536]{1,0:T(8,128)S(1)}, f32[128,1536]{1,0:T(8,128)S(1)}, u32[]{:S(2)}, u32[]{:S(2)}) collective-permute-start(f32[128,1536]{1,0:T(8,128)S(1)} %fusion.7), channel_id=1, source_target_pairs={{0,8},{8,0},{1,9},{9,1},{2,10},{10,2},{3,11},{11,3},{4,12},{12,4},... | collective-permute-start | bytes 2359304 | tf_op jit(solution)/shard_map/ppermute | solution.py:210
Sparse Core Ops, SparseCore 0:
  65.4 45.3 all-gather.3

commit v2 on v0

v2 whole, which is shorter than its diff:
```python
import functools
import math

import jax
import jax.numpy as jnp
from jax import lax
from jax.experimental import pallas as pl
from jax.experimental.pallas import tpu as pltpu
from jax.sharding import PartitionSpec as P

VALID_CLASSES = 21841
LN_EPS = 1e-5
SMOOTH = 0.1
LANES = 128
COLS = 512
SUB = 256
IMGS = 8
ROW_TILE = 16
GROUP = 4
WCOLS = 1024
SLOTS = 3


def repeat_lanes(tile, width):
    return jnp.concatenate([tile] * (width // LANES), axis=1)


def fold_lanes(x, op):
    tiles = [x[:, j * LANES:(j + 1) * LANES] for j in range(x.shape[1] // LANES)]
    return functools.reduce(op, tiles)


def spread_row(row):
    return jnp.broadcast_to(row, (LANES, LANES)).T


def norm_image(x_ref, slot, i, lane_id, pool_row, pool_ref, mean_ref, inv_ref):
    _, _, tokens, width = x_ref.shape
    chunks = tokens // ROW_TILE
    lane = lax.broadcasted_iota(jnp.int32, (ROW_TILE, LANES), 1)
    means, invs = [], []
    for c in range(chunks):
        x = x_ref[slot, i, pl.ds(c * ROW_TILE, ROW_TILE), :].astype(jnp.float32)
        means.append(jnp.sum(x, axis=1, keepdims=True) * (1.0 / width))
    for c in range(chunks):
        x = x_ref[slot, i, pl.ds(c * ROW_TILE, ROW_TILE), :].astype(jnp.float32) - means[c]
        var = jnp.sum(x * x, axis=1, keepdims=True) * (1.0 / width)
        invs.append(lax.rsqrt(var + LN_EPS))
    total = jnp.zeros((ROW_TILE, width), jnp.float32)
    shift = jnp.zeros((ROW_TILE, 1), jnp.float32)
    for c in range(chunks):
        x = x_ref[slot, i, pl.ds(c * ROW_TILE, ROW_TILE), :].astype(jnp.float32)
        total = total + x * invs[c]
        shift = shift + means[c] * invs[c]
        rows = pl.ds(c * ROW_TILE, ROW_TILE)
        mean_ref[rows, :] = jnp.where(lane == lane_id, means[c], mean_ref[rows, :])
        inv_ref[rows, :] = jnp.where(lane == lane_id, invs[c], inv_ref[rows, :])
    pool_ref[pl.ds(pool_row, 1), :] = jnp.sum(total - shift, axis=0, keepdims=True) * (1.0 / tokens)


def front_kernel(x_hbm, w_hbm, b_ref, gamma_ref, beta_ref, y_ref,
                 pool_out, mean_ref, inv_ref, dpool_ref, lse_ref, loss_ref, dgb_ref,
                 x_buf, w_buf, pool, logits, p16, stat_send, stat_recv, part, part_all, mi_send, mi_recv,
                 x_sem, w_sem, send_sem, recv_sem, st_send_sem, st_recv_sem, dg_send_sem, dg_recv_sem, out_sem):
    rows, tokens, width = x_hbm.shape
    half = rows // 2
    quarter = half // 2
    shard_cols = w_hbm.shape[1]
    n_w = shard_cols // WCOLS
    groups = half // GROUP
    rows_total = pool.shape[0]
    t = lax.axis_index("tp")
    d = lax.axis_index("dp")
    me = t * 8 + d
    dx = d + 2 - 4 * ((d // 2) % 2)
    dy = d + 4 - 8 * (d // 4)
    dxy = dx + 4 - 8 * (d // 4)

    def sibling(q):
        return q + 1 - 2 * (q % 2)

    def peer(k):
        q = (me + k) % 16
        return {"tp": q // 8, "dp": q % 8}

    barrier = pltpu.get_barrier_semaphore()
    for k in range(1, 16):
        pl.semaphore_signal(barrier, inc=1, device_id=peer(k), device_id_type=pl.DeviceIdType.MESH)

    def x_copy(g, slot):
        return pltpu.make_async_copy(x_hbm.at[pl.ds(t * half + g * GROUP, GROUP)], x_buf.at[slot], x_sem.at[slot])

    def w_copy(k):
        return pltpu.make_async_copy(w_hbm.at[:, pl.ds(k * WCOLS, WCOLS)], w_buf.at[k], w_sem.at[k])

    def chunk(q, tt, h):
        return pool.at[pl.ds(q * rows + tt * half + h * quarter, quarter)]

    def remote(ref, sem, target):
        return pltpu.make_async_remote_copy(src_ref=ref, dst_ref=ref, send_sem=send_sem.at[sem], recv_sem=recv_sem.at[sem], device_id=target, device_id_type=pl.DeviceIdType.MESH)

    to_z = {"tp": 1 - t, "dp": d}
    to_x = {"tp": t, "dp": dx}
    to_y = {"tp": t, "dp": dy}
    to_c = {"tp": t, "dp": sibling(d)}

    x_copy(0, 0).start()
    x_copy(1, 1).start()
    mean_ref[...] = jnp.zeros_like(mean_ref)
    inv_ref[...] = jnp.zeros_like(inv_ref)

    def do_group(g, carry):
        slot = g % SLOTS
        x_copy(g, slot).wait()

        @pl.when(g + 2 < groups)
        def _():
            x_copy(g + 2, (g + 2) % SLOTS).start()

        @pl.when(g < n_w)
        def _():
            w_copy(g).start()

        def image(i, c):
            local = t * half + g * GROUP + i
            norm_image(x_buf, slot, i, local, d * rows + local, pool, mean_ref, inv_ref)
            return c

        lax.fori_loop(0, GROUP, image, 0)
        return carry

    lax.fori_loop(0, groups // 2, do_group, 0)
    pl.semaphore_wait(barrier, 15)
    first = [[remote(chunk(d, t, h), 3 * h + j, to) for j, to in enumerate((to_z, to_x, to_y))] for h in range(2)]
    for c in first[0]:
        c.start()
    lax.fori_loop(groups // 2, groups, do_group, 0)
    mi_send[0] = mean_ref[...]
    mi_send[1] = inv_ref[...]
    for c in first[1]:
        c.start()
    mi_copy = pltpu.make_async_remote_copy(src_ref=mi_send, dst_ref=mi_recv, send_sem=send_sem.at[18], recv_sem=recv_sem.at[18], device_id=to_z, device_id_type=pl.DeviceIdType.MESH)
    second = [[remote(chunk(d, 1 - t, h), 6 + 2 * h + j, to) for j, to in enumerate((to_x, to_y))] for h in range(2)]
    third = [[remote(chunk(dx, t, h), 10 + 2 * h, to_y), remote(chunk(dy, 1 - t, h), 11 + 2 * h, to_x)] for h in range(2)]

    def block(q):
        return pool.at[pl.ds(q * rows, rows)]

    fourth = [remote(block(q), 14 + j, to_c) for j, q in enumerate((d, dx, dy, dxy))]
    for h in range(2):
        first[h][0].wait_recv()
        for c in second[h]:
            c.start()
    fourth[0].start()
    mi_copy.start()

    p16[...] = (pool[pl.ds(d * rows, rows), :] * gamma_ref[...] + beta_ref[...]).astype(jnp.bfloat16)

    def col_ids(k):
        return t * shard_cols + k * WCOLS + lax.broadcasted_iota(jnp.int32, (1, WCOLS), 1)

    def logits_step(k, top):
        w_copy(k).wait()
        cols = col_ids(k)
        bias = jnp.where(cols < VALID_CLASSES, b_ref[k], -jnp.inf)
        out = jnp.dot(p16[...], w_buf[k], preferred_element_type=jnp.float32) + bias
        logits[k] = out
        return jnp.maximum(top, fold_lanes(out, jnp.maximum))

    top = lax.fori_loop(0, n_w, logits_step, jnp.full((rows, LANES), -jnp.inf, jnp.float32))
    for h in range(2):
        first[h][1].wait_recv()
        third[h][0].start()
    for h in range(2):
        second[h][1].wait_recv()
        third[h][1].start()
    for h in range(2):
        second[h][0].wait_recv()
        first[h][2].wait_recv()
    fourth[1].start()
    fourth[2].start()
    row_top = jnp.broadcast_to(jnp.max(top, axis=1, keepdims=True), (rows, LANES))
    labels = y_ref[...]
    zero = jnp.zeros((rows, LANES), jnp.float32)

    def stat_step(k, carry):
        total, target, valid_sum = carry
        cols = col_ids(k)
        out = logits[k]
        e = jnp.exp(out - repeat_lanes(row_top, WCOLS))
        hit = jnp.where(repeat_lanes(labels, WCOLS) == cols, out, 0.0)
        ok = jnp.where(cols < VALID_CLASSES, out, 0.0)
        return total + fold_lanes(e, jnp.add), target + fold_lanes(hit, jnp.add), valid_sum + fold_lanes(ok, jnp.add)

    total, target, valid_sum = lax.fori_loop(0, n_w, stat_step, (zero, zero, zero))
    lane = lax.broadcasted_iota(jnp.int32, (rows, LANES), 1)
    packed = jnp.where(lane == 0, row_top, jnp.where(lane == 1, jnp.sum(total, axis=1, keepdims=True), jnp.where(lane == 2, jnp.sum(target, axis=1, keepdims=True), jnp.sum(valid_sum, axis=1, keepdims=True))))
    stat_send[...] = packed.T[:8]
    stat_recv[me] = stat_send[...]

    def stat_copy(k):
        return pltpu.make_async_remote_copy(src_ref=stat_send, dst_ref=stat_recv.at[me], send_sem=st_send_sem.at[k - 1], recv_sem=st_recv_sem.at[k - 1], device_id=peer(k), device_id_type=pl.DeviceIdType.MESH)

    stat_copies = [stat_copy(k) for k in range(1, 16)]
    for c in stat_copies:
        c.start()
    for c in stat_copies:
        c.wait()

    def lse_of(q):
        a, b = stat_recv[q], stat_recv[8 + q]
        hi = jnp.maximum(a[0:1], b[0:1])
        return hi + jnp.log(a[1:2] * jnp.exp(a[0:1] - hi) + b[1:2] * jnp.exp(b[0:1] - hi))

    loss = jnp.zeros((1, LANES), jnp.float32)
    for q in range(8):
        lse_q = lse_of(q)
        lse_ref[q:q + 1, :] = lse_q
        a, b = stat_recv[q], stat_recv[8 + q]
        loss = loss + lse_q - (1.0 - SMOOTH) * (a[2:3] + b[2:3]) - (SMOOTH / VALID_CLASSES) * (a[3:4] + b[3:4])
    loss_ref[...] = jnp.broadcast_to(loss, loss_ref.shape)
    lse_own = spread_row(lse_of(d))
    dpool_ref[...] = jnp.zeros_like(dpool_ref)

    def dpool_step(k, carry):
        cols = col_ids(k)
        smooth = jnp.where(cols < VALID_CLASSES, SMOOTH / VALID_CLASSES, 0.0)
        soft = jnp.exp(logits[k] - repeat_lanes(lse_own, WCOLS))
        dl = (soft - jnp.where(repeat_lanes(labels, WCOLS) == cols, smooth + (1.0 - SMOOTH), smooth)) * (1.0 / rows_total)
        dpool_ref[...] += lax.dot_general(dl.astype(jnp.bfloat16), w_buf[k], (((1,), (1,)), ((), ())), preferred_element_type=jnp.float32)
        return carry

    lax.fori_loop(0, n_w, dpool_step, 0)
    for h in range(2):
        third[h][0].wait_recv()
        third[h][1].wait_recv()
    fourth[3].start()
    dpool = dpool_ref[...]
    part[0:1, :] = jnp.sum(dpool * pool[pl.ds(d * rows, rows), :], axis=0, keepdims=True)
    part[1:2, :] = jnp.sum(dpool, axis=0, keepdims=True)
    part_all[me] = part[...]

    def part_copy(k):
        return pltpu.make_async_remote_copy(src_ref=part, dst_ref=part_all.at[me], send_sem=dg_send_sem.at[k - 1], recv_sem=dg_recv_sem.at[k - 1], device_id=peer(k), device_id_type=pl.DeviceIdType.MESH)

    part_copies = [part_copy(k) for k in range(1, 16)]
    for c in part_copies:
        c.start()
    mi_copy.wait()
    lane_t = lax.broadcasted_iota(jnp.int32, (tokens, LANES), 1)
    mine = lane_t // half == t
    mean_ref[...] = jnp.where(mine, mean_ref[...], mi_recv[0])
    inv_ref[...] = jnp.where(mine, inv_ref[...], mi_recv[1])
    for c in fourth:
        c.wait_recv()
    flush = pltpu.make_async_copy(pool, pool_out, out_sem)
    flush.start()
    for c in part_copies:
        c.wait()
    dgb_ref[...] = jnp.sum(part_all[...], axis=0)
    for c in first[0] + first[1] + second[0] + second[1] + third[0] + third[1] + fourth:
        c.wait_send()
    flush.wait()


def front_call(feats, w_head, b_head, ln_gamma, ln_beta, labels, n_data):
    rows, tokens, width = feats.shape
    shard_cols = w_head.shape[1]
    n_w = shard_cols // WCOLS
    f32 = jnp.float32
    vmem = pl.BlockSpec(memory_space=pltpu.VMEM)
    anym = pl.BlockSpec(memory_space=pl.ANY)
    stat = jax.ShapeDtypeStruct((tokens, LANES), f32)
    return pl.pallas_call(
        front_kernel,
        name="front",
        in_specs=[anym, anym, vmem, vmem, vmem, vmem],
        out_specs=[anym, vmem, vmem, vmem, vmem, vmem, vmem],
        out_shape=[
            jax.ShapeDtypeStruct((rows * n_data, width), f32),
            stat,
            stat,
            jax.ShapeDtypeStruct((rows, width), f32),
            jax.ShapeDtypeStruct((8, LANES), f32),
            jax.ShapeDtypeStruct((8, LANES), f32),
            jax.ShapeDtypeStruct((2, width), f32),
        ],
        scratch_shapes=[
            pltpu.VMEM((SLOTS, GROUP, tokens, width), jnp.bfloat16),
            pltpu.VMEM((n_w, width, WCOLS), jnp.bfloat16),
            pltpu.VMEM((rows * n_data, width), f32),
            pltpu.VMEM((n_w, rows, WCOLS), f32),
            pltpu.VMEM((rows, width), jnp.bfloat16),
            pltpu.VMEM((8, LANES), f32),
            pltpu.VMEM((16, 8, LANES), f32),
            pltpu.VMEM((2, width), f32),
            pltpu.VMEM((16, 2, width), f32),
            pltpu.VMEM((2, tokens, LANES), f32),
            pltpu.VMEM((2, tokens, LANES), f32),
            pltpu.SemaphoreType.DMA((SLOTS,)),
            pltpu.SemaphoreType.DMA((n_w,)),
            pltpu.SemaphoreType.DMA((19,)),
            pltpu.SemaphoreType.DMA((19,)),
            pltpu.SemaphoreType.DMA((15,)),
            pltpu.SemaphoreType.DMA((15,)),
            pltpu.SemaphoreType.DMA((15,)),
            pltpu.SemaphoreType.DMA((15,)),
            pltpu.SemaphoreType.DMA,
        ],
        compiler_params=pltpu.CompilerParams(collective_id=0, has_side_effects=True, vmem_limit_bytes=63 * 2**20),
    )(feats, w_head, b_head.reshape(n_w, 1, WCOLS), ln_gamma[None, :], ln_beta[None, :], jnp.broadcast_to(labels[:, None], (rows, LANES)))


def head_kernel(shard_cols, pool_ref, gamma_ref, beta_ref, lse_ref, y_ref, w_ref, b_ref, dw_ref, db_ref, p_ref, pt_ref, lse_b, y_b, dl_ref):
    block = pl.program_id(0)
    rows, width = p_ref.shape

    @pl.when(block == 0)
    def _():
        def fill(r, carry):
            sl = pl.ds(r * LANES, LANES)
            p = pool_ref[sl, :] * gamma_ref[...] + beta_ref[...]
            p_ref[sl, :] = p.astype(jnp.bfloat16)
            lse_b[sl, :] = spread_row(lse_ref[pl.ds(r, 1), :])
            y_b[sl, :] = spread_row(y_ref[pl.ds(r, 1), :])
            return carry

        lax.fori_loop(0, rows // LANES, fill, 0)
        for r in range(rows // LANES):
            pt_ref[:, r * LANES:(r + 1) * LANES] = p_ref[r * LANES:(r + 1) * LANES, :].T

    base = lax.axis_index("tp") * shard_cols + block * COLS
    for s in range(COLS // SUB):
        sub = pl.ds(s * SUB, SUB)
        logits = jnp.dot(p_ref[...], w_ref[:, sub], preferred_element_type=jnp.float32)
        col = base + s * SUB + lax.broadcasted_iota(jnp.int32, (1, SUB), 1)
        valid = col < VALID_CLASSES
        smooth = jnp.where(valid, SMOOTH / VALID_CLASSES, 0.0)
        target = smooth + (1.0 - SMOOTH)
        bias = jnp.where(valid, b_ref[:, sub], -jnp.inf)
        soft = jnp.exp((logits + bias) - repeat_lanes(lse_b[...], SUB))
        dlogit = (soft - jnp.where(repeat_lanes(y_b[...], SUB) == col, target, smooth)) * (1.0 / rows)
        db_ref[:, sub] = jnp.sum(dlogit, axis=0, keepdims=True)
        dl_ref[s] = dlogit.astype(jnp.bfloat16)
    for s in range(COLS // SUB):
        dw_ref[:, pl.ds(s * SUB, SUB)] = jnp.dot(pt_ref[...], dl_ref[s], preferred_element_type=jnp.float32)


def resident(shape):
    return pl.BlockSpec(shape, lambda g: (0,) * len(shape), pipeline_mode=pl.Buffered(1))


def head_call(pool, ln_gamma, ln_beta, lse_all, y_all, w_head, b_head):
    rows, width = pool.shape
    shard_cols = w_head.shape[1]
    steps = shard_cols // COLS
    dw, db = pl.pallas_call(
        functools.partial(head_kernel, shard_cols),
        name="head",
        grid=(steps,),
        in_specs=[
            resident((rows, width)),
            resident((1, width)),
            resident((1, width)),
            resident((8, LANES)),
            resident((8, LANES)),
            pl.BlockSpec((width, COLS), lambda g: (0, g)),
            pl.BlockSpec((1, COLS), lambda g: (0, g)),
        ],
        out_specs=[pl.BlockSpec((width, COLS), lambda g: (0, g)), pl.BlockSpec((1, COLS), lambda g: (0, g))],
        out_shape=[jax.ShapeDtypeStruct((width, shard_cols), jnp.float32), jax.ShapeDtypeStruct((1, shard_cols), jnp.float32)],
        scratch_shapes=[
            pltpu.VMEM((rows, width), jnp.bfloat16),
            pltpu.VMEM((width, rows), jnp.bfloat16),
            pltpu.VMEM((rows, LANES), jnp.float32),
            pltpu.VMEM((rows, LANES), jnp.int32),
            pltpu.VMEM((COLS // SUB, rows, SUB), jnp.bfloat16),
        ],
        compiler_params=pltpu.CompilerParams(vmem_limit_bytes=48 * 2**20),
        cost_estimate=pl.CostEstimate(flops=4 * rows * width * shard_cols, bytes_accessed=6 * width * shard_cols, transcendentals=rows * shard_cols),
    )(pool, ln_gamma[None, :], ln_beta[None, :], lse_all, y_all, w_head, b_head[None, :])
    return dw, db[0]


def feat_kernel(x_ref, mean_ref, inv_ref, own_ref, other_ref, gamma_ref, df_ref):
    imgs, tokens, width = x_ref.shape
    chunks = tokens // ROW_TILE
    turn = (LANES - pl.program_id(0) * IMGS) % LANES
    u_all = (own_ref[...] + other_ref[...]) * gamma_ref[...] * (1.0 / tokens)
    us_all = jnp.sum(u_all, axis=1, keepdims=True)
    for i in range(imgs):
        u = u_all[i:i + 1, :]
        us = us_all[i:i + 1, :]
        um = us * (1.0 / width)
        for c in range(chunks):
            rows = pl.ds(c * ROW_TILE, ROW_TILE)
            mean = pltpu.roll(mean_ref[rows, :], turn, axis=1)[:, i:i + 1]
            inv = pltpu.roll(inv_ref[rows, :], turn, axis=1)[:, i:i + 1]
            x = x_ref[i, rows, :].astype(jnp.float32)
            proj = (jnp.sum(x * u, axis=1, keepdims=True) - mean * us) * (inv * (1.0 / width))
            slope = -(inv * inv * proj)
            offset = -(inv * um) - slope * mean
            x = x_ref[i, rows, :].astype(jnp.float32)
            df_ref[i, rows, :] = (x * slope + (u * inv + offset)).astype(jnp.bfloat16)


def feat_call(feats, mean, inv, own, other, ln_gamma):
    rows, tokens, width = feats.shape
    img = lambda shape: pl.BlockSpec(shape, lambda g: (g,) + (0,) * (len(shape) - 1))
    return pl.pallas_call(
        feat_kernel,
        name="feat",
        grid=(rows // IMGS,),
        in_specs=[img((IMGS, tokens, width)), resident((tokens, LANES)), resident((tokens, LANES)), img((IMGS, width)), img((IMGS, width)), resident((1, width))],
        out_specs=img((IMGS, tokens, width)),
        out_shape=jax.ShapeDtypeStruct(feats.shape, jnp.bfloat16),
        compiler_params=pltpu.CompilerParams(vmem_limit_bytes=48 * 2**20),
        cost_estimate=pl.CostEstimate(flops=10 * rows * tokens * width, bytes_accessed=4 * rows * tokens * width, transcendentals=0),
    )(feats, mean, inv, own, other, ln_gamma[None, :])


def solution(mesh):
    n_data = mesh.shape["dp"]

    def local_head(feats, ln_gamma, ln_beta, w_head, b_head, labels):
        rows = feats.shape[0]
        y_all = lax.all_gather(labels, "dp", axis=0, tiled=False)
        pool, mean, inv, dpool, lse_all, loss, dgb = front_call(feats, w_head, b_head, ln_gamma, ln_beta, labels, n_data)
        dpool_other = lax.ppermute(dpool, "tp", [(0, 1), (1, 0)])
        dw, db = head_call(pool, ln_gamma, ln_beta, lse_all, y_all, w_head, b_head)
        df = feat_call(feats, mean, inv, dpool, dpool_other, ln_gamma)
        return jnp.sum(loss[0]) / (rows * n_data), df, dw, db, dgb[0], dgb[1]

    return jax.shard_map(local_head, mesh=mesh, in_specs=(P("dp", None, None), P(), P(), P(None, "tp"), P("tp"), P("dp")), out_specs=(P(), P("dp", None, None), P(None, "tp"), P("tp"), P(), P()), check_vma=False)
```

time: 1040 us -> 243 us (0.23)
  waiting for transfers between devices: 687 us -> 0.01 us
  Pallas kernels: 0 us -> 225 us
  other arithmetic: 192 us -> 1.28 us
  matrix products: 65.9 us -> 0 us
  local copies, waits for them, and re-layouts: 44.4 us -> 5.34 us
  blocking collectives: 36 us -> 8.66 us
  between operations: 16 us -> 2.47 us
    psum x2 -> x0, waiting for transfers between devices: 687 us -> none  [the longest x1 687 us: local_head(): lax.psum(lax.dot_general(pooled16, dlogit16, (((0,), (0,)), ((), ())), pr...]
    pallas_call x0 -> x3, Pallas kernels: none -> 225 us  [the longest x1 89.6 us: head_call(): pl.pallas_call(functools.partial(head_kernel, shard_cols), name='head', g...]
    reduce_sum x8 -> x1, other arithmetic: 154 us -> 1.28 us  [local_head(): return (jnp.sum(loss[0]) / (rows * n_data), df, dw, db, dgb[0], dgb[1])]
    dot_general x3 -> x0, matrix products: 65.9 us -> none  [the longest x1 28.8 us: local_head(): lax.dot_general(pooled16, dlogit16, (((0,), (0,)), ((), ())), preferred_e...]
    unnamed x9 -> x18, local copies, waits for them, and re-layouts: 44.4 us -> 0.71 us
    convert_element_type x1 -> x0, other arithmetic: 37.6 us -> none  [norm_backward(): return (grad_x.astype(jnp.bfloat16), grad_gamma, grad_beta)]
    psum x2 -> x0, blocking collectives: 29.8 us -> none  [the longest x1 24.6 us: local_head(): lax.psum((jnp.sum(loss_rows), grad_gamma, grad_beta), 'dp')]
  transfers between devices with their start and end apart: 2 -> 1, of which waited for: 1 -> 0; matrix products, arithmetic and copies ran while one was open for 10% -> 1% of each run, Pallas kernels for 0% -> 37%
where the time goes in v2:
time: 243 us
  Pallas kernels  225 us (93%)
  blocking collectives  8.66 us (4%)
  local copies, waits for them, and re-layouts  5.34 us (2%)
  between operations  2.47 us (1%)
    pallas_call x1, Pallas kernels, head_call(): pl.pallas_call(functools.partial(head_kernel, shard_cols), name='head', g...  89.6 us
    pallas_call x1, Pallas kernels, front_call(): pl.pallas_call(front_kernel, name='front', in_specs=[anym, anym, vmem, vm...  71.5 us
    pallas_call x1, Pallas kernels, feat_call(): pl.pallas_call(feat_kernel, name='feat', grid=(rows // IMGS,), in_specs=[...  63.4 us
    all_gather x1, blocking collectives, local_head(): y_all = lax.all_gather(labels, 'dp', axis=0, tiled=False)  8.66 us
  transfers between devices with their start and end apart: 1, of which 0 were waited for; matrix products, arithmetic and copies ran while one was open for 1% of the time, Pallas kernels for 37%

profile of v2, /device:TPU:0, one launch (start us, length us, event | category | flops | bytes accessed | tf_op | source)
XLA Modules:
  0.0 243.0 jit_solution(1413073471683187678)
XLA Ops:
  0.6 0.0 copy-start.4
  0.6 0.0 copy-start.8
  0.7 1.3 broadcast_in_dim.8.gamma_ref
  2.0 0.0 copy-start.3
  2.0 1.3 broadcast_in_dim.9.beta_ref
  3.3 0.0 copy-start.5
  3.3 1.4 broadcast_in_dim.20.y_ref
  4.7 71.5 %front.1 = (f32[1024,1536]{1,0:T(8,128)}, f32[144,128]{1,0:T(8,128)}, f32[144,128]{1,0:T(8,128)}, f32[128,1536]{1,0:T(8,128)}, f32[8,128]{1,0:T(8,128)}, /*index=5*/f32[8,128]{1,0:T(8,128)}, f32[2,1536]{1,0:T(2,128)}) custom-call(bf16[128,144,1536]{2,1,0:T(8,128)(2,1)} %x_ref.1, bf16[1536,11264]{1,0:T(8,128)(2,1)} %w_ref.1, f32[11,1,1024]{2,1,0:T(1,128)} %bitcast.5, ...), custom_call_target="tpu_custom_call" | custom-call | tf_op jit(solution)/shard_map/front/pallas_call | solution.py:274
  76.2 0.7 collective-permute-start
  76.9 0.0 copy-done.8
  76.9 8.7 %all-gather.1 = s32[8,1,128]{2,1,0:T(1,128)S(1)} all-gather(s32[1,1,128]{2,1,0:T(1,128)S(1)} %bitcast.8), channel_id=2, replica_groups=mesh['tp'=2,'dp'=8] {'dp'}, dimensions={0}, use_global_device_ids=true | all-gather | bytes 4608 | tf_op jit(solution)/shard_map/all_gather | solution.py:427
  85.6 0.0 copy-done.4
  85.6 0.0 copy-done.3
  85.6 0.0 copy-done.5
  85.6 0.7 copy-done.6
  86.3 89.6 %head.1 = (f32[1536,11264]{1,0:T(8,128)}, f32[1,11264]{1,0:T(1,128)}) custom-call(f32[1024,1536]{1,0:T(8,128)} %get-tuple-element.19.pool_ref, f32[1,1536]{1,0:T(1,128)S(1)} %copy-done.3, f32[1,1536]{1,0:T(1,128)S(1)} %copy-done.5, f32[8,128]{1,0:T(8,128)S(1)} %copy-done.6, s32[8,128]{1,0:T(8,128)S(1)} %bitcast.7, bf16[1536,11264]{1,0:T(8,128)(2,1)} %w_ref.1, ...), custom_call_target="tpu_custom_call" | custom-call | flops 70866960384 | bytes 103809024 | tf_op jit(solution)/shard_map/head/pallas_call | solution.py:357
  175.9 1.3 slice_reduce_fusion.2
  177.8 0.0 copy-done.7
  177.8 0.6 slice_reduce_fusion
  178.4 0.0 collective-permute-done.other_ref
  178.4 0.0 copy-done
  178.5 0.0 copy-done.1
  178.5 0.0 copy-done.2
  178.5 63.4 %feat.1 = bf16[128,144,1536]{2,1,0:T(8,128)(2,1)} custom-call(bf16[128,144,1536]{2,1,0:T(8,128)(2,1)} %x_ref.1, f32[144,128]{1,0:T(8,128)S(1)} %copy-done.1, f32[144,128]{1,0:T(8,128)S(1)} %copy-done.2, f32[128,1536]{1,0:T(8,128)S(1)} %copy-done, f32[128,1536]{1,0:T(8,128)S(1)} %collective-permute-done.other_ref, f32[1,1536]{1,0:T(1,128)S(1)} %copy-done.3), custom_call_target="tpu_custom_call" | custom-call | flops 283115520 | bytes 113246208 | tf_op jit(solution)/shard_map/feat/pallas_call | solution.py:410
  (5 shorter events, 0.0 us)
Async XLA Ops:
  0.6 85.0 %copy-start.4 = (f32[11264]{0:T(1024)S(1)}, f32[11264]{0:T(1024)}, u32[]{:S(2)}) copy-start(f32[11264]{0:T(1024)} %param.10) | copy-start | bytes 135172
  0.6 76.3 %copy-start.8 = (s32[128]{0:T(128)S(1)}, s32[128]{0:T(128)}, u32[]{:S(2)}) copy-start(s32[128]{0:T(128)} %param.11) | copy-start | bytes 1540
  2.0 83.6 %copy-start.3 = (f32[1,1536]{1,0:T(1,128)S(1)}, f32[1,1536]{1,0:T(1,128)}, u32[]{:S(2)}) copy-start(f32[1,1536]{1,0:T(1,128)} %broadcast_in_dim.8.gamma_ref) | copy-start | bytes 18436
  3.3 82.3 %copy-start.5 = (f32[1,1536]{1,0:T(1,128)S(1)}, f32[1,1536]{1,0:T(1,128)}, u32[]{:S(2)}) copy-start(f32[1,1536]{1,0:T(1,128)} %broadcast_in_dim.9.beta_ref) | copy-start | bytes 18436
  76.2 102.3 %collective-permute-start = (f32[128,1536]{1,0:T(8,128)}, f32[128,1536]{1,0:T(8,128)S(1)}, u32[]{:S(2)}, u32[]{:S(2)}) collective-permute-start(f32[128,1536]{1,0:T(8,128)} %get-tuple-element.18.own_ref), channel_id=1, source_target_pairs={{0,8},{8,0},{1,9},{9,1},{2,10},{10,2},{3,11},{11,3},{4,12},{12,4},... | collective-permute-start | bytes 2359304 | tf_op jit(solution)/shard_map/ppermute | solution.py:429
  85.6 0.7 copy-start.6
  86.3 91.5 %copy-start.7 = (f32[2,1536]{1,0:T(2,128)S(1)}, f32[2,1536]{1,0:T(2,128)}, u32[]{:S(2)}) copy-start(f32[2,1536]{1,0:T(2,128)} %get-tuple-element.23) | copy-start | bytes 36868
  86.3 92.1 %copy-start = (f32[128,1536]{1,0:T(8,128)S(1)}, f32[128,1536]{1,0:T(8,128)}, u32[]{:S(2)}) copy-start(f32[128,1536]{1,0:T(8,128)} %get-tuple-element.18.own_ref) | copy-start | bytes 2359300
  86.3 92.2 %copy-start.1 = (f32[144,128]{1,0:T(8,128)S(1)}, f32[144,128]{1,0:T(8,128)}, u32[]{:S(2)}) copy-start(f32[144,128]{1,0:T(8,128)} %get-tuple-element.16.mean_ref) | copy-start | bytes 221188
  86.3 92.2 %copy-start.2 = (f32[144,128]{1,0:T(8,128)S(1)}, f32[144,128]{1,0:T(8,128)}, u32[]{:S(2)}) copy-start(f32[144,128]{1,0:T(8,128)} %get-tuple-element.17.inv_ref) | copy-start | bytes 221188

commit v3 on v2

--- a/solution.py
+++ b/solution.py
@@ -12,13 +12,14 @@
 LN_EPS = 1e-5
 SMOOTH = 0.1
 LANES = 128
-COLS = 512
+COLS = 1024
 SUB = 256
 IMGS = 8
 ROW_TILE = 16
 GROUP = 4
 WCOLS = 1024
 SLOTS = 3
+PIECES = 4
 
 
 def repeat_lanes(tile, width):
@@ -59,12 +60,12 @@
 
 
 def front_kernel(x_hbm, w_hbm, b_ref, gamma_ref, beta_ref, y_ref,
-                 pool_out, mean_ref, inv_ref, dpool_ref, lse_ref, loss_ref, dgb_ref,
+                 pool_out, mean_ref, inv_ref, dpool_ref, lse_ref, yf_ref, loss_ref, dgamma_ref, dbeta_ref,
                  x_buf, w_buf, pool, logits, p16, stat_send, stat_recv, part, part_all, mi_send, mi_recv,
                  x_sem, w_sem, send_sem, recv_sem, st_send_sem, st_recv_sem, dg_send_sem, dg_recv_sem, out_sem):
     rows, tokens, width = x_hbm.shape
     half = rows // 2
-    quarter = half // 2
+    quarter = half // PIECES
     shard_cols = w_hbm.shape[1]
     n_w = shard_cols // WCOLS
     groups = half // GROUP
@@ -117,9 +118,9 @@
         def _():
             x_copy(g + 2, (g + 2) % SLOTS).start()
 
-        @pl.when(g < n_w)
+        @pl.when(g % 3 != 2)
         def _():
-            w_copy(g).start()
+            w_copy(g - g // 3).start()
 
         def image(i, c):
             local = t * half + g * GROUP + i
@@ -129,32 +130,53 @@
         lax.fori_loop(0, GROUP, image, 0)
         return carry
 
-    lax.fori_loop(0, groups // 2, do_group, 0)
-    pl.semaphore_wait(barrier, 15)
-    first = [[remote(chunk(d, t, h), 3 * h + j, to) for j, to in enumerate((to_z, to_x, to_y))] for h in range(2)]
-    for c in first[0]:
-        c.start()
-    lax.fori_loop(groups // 2, groups, do_group, 0)
-    mi_send[0] = mean_ref[...]
-    mi_send[1] = inv_ref[...]
-    for c in first[1]:
-        c.start()
-    mi_copy = pltpu.make_async_remote_copy(src_ref=mi_send, dst_ref=mi_recv, send_sem=send_sem.at[18], recv_sem=recv_sem.at[18], device_id=to_z, device_id_type=pl.DeviceIdType.MESH)
-    second = [[remote(chunk(d, 1 - t, h), 6 + 2 * h + j, to) for j, to in enumerate((to_x, to_y))] for h in range(2)]
-    third = [[remote(chunk(dx, t, h), 10 + 2 * h, to_y), remote(chunk(dy, 1 - t, h), 11 + 2 * h, to_x)] for h in range(2)]
+    first = [[remote(chunk(d, t, j), 3 * j + a, to) for a, to in enumerate((to_z, to_x, to_y))] for j in range(PIECES)]
+    second = [[remote(chunk(d, 1 - t, j), 12 + 2 * j + a, to) for a, to in enumerate((to_x, to_y))] for j in range(PIECES)]
+    third = [[remote(chunk(dx, t, j), 20 + 2 * j, to_y), remote(chunk(dy, 1 - t, j), 21 + 2 * j, to_x)] for j in range(PIECES)]
 
     def block(q):
         return pool.at[pl.ds(q * rows, rows)]
 
-    fourth = [remote(block(q), 14 + j, to_c) for j, q in enumerate((d, dx, dy, dxy))]
-    for h in range(2):
-        first[h][0].wait_recv()
-        for c in second[h]:
+    fourth = [remote(block(q), 28 + j, to_c) for j, q in enumerate((d, dx, dy, dxy))]
+    mi_copy = pltpu.make_async_remote_copy(src_ref=mi_send, dst_ref=mi_recv, send_sem=send_sem.at[32], recv_sem=recv_sem.at[32], device_id=to_z, device_id_type=pl.DeviceIdType.MESH)
+
+    def flush(j, q):
+        return pltpu.make_async_copy(block(q), pool_out.at[pl.ds(q * rows, rows)], out_sem.at[j])
+
+    flushes = [flush(j, q) for j, q in enumerate((d, dx, dy, dxy, sibling(d), sibling(dx), sibling(dy), sibling(dxy)))]
+
+    def pass_z(j):
+        first[j][0].wait_recv()
+        for c in second[j]:
             c.start()
+
+    def pass_x(j):
+        first[j][1].wait_recv()
+        third[j][0].start()
+
+    def pass_y(j):
+        second[j][1].wait_recv()
+        third[j][1].start()
+
+    for j in range(PIECES):
+        lax.fori_loop(j * groups // PIECES, (j + 1) * groups // PIECES, do_group, 0)
+        if j == 0:
+            pl.semaphore_wait(barrier, 15)
+        if j == PIECES - 1:
+            mi_send[0] = mean_ref[...]
+            mi_send[1] = inv_ref[...]
+        for c in first[j]:
+            c.start()
+        if j >= 1:
+            pass_z(j - 1)
+            pass_x(j - 1)
+        if j >= 2:
+            pass_y(j - 2)
+    pass_z(PIECES - 1)
     fourth[0].start()
-    mi_copy.start()
-
-    p16[...] = (pool[pl.ds(d * rows, rows), :] * gamma_ref[...] + beta_ref[...]).astype(jnp.bfloat16)
+    gamma = gamma_ref[...].reshape(1, width)
+    beta = beta_ref[...].reshape(1, width)
+    p16[...] = (pool[pl.ds(d * rows, rows), :] * gamma + beta).astype(jnp.bfloat16)
 
     def col_ids(k):
         return t * shard_cols + k * WCOLS + lax.broadcasted_iota(jnp.int32, (1, WCOLS), 1)
@@ -167,20 +189,20 @@
         logits[k] = out
         return jnp.maximum(top, fold_lanes(out, jnp.maximum))
 
-    top = lax.fori_loop(0, n_w, logits_step, jnp.full((rows, LANES), -jnp.inf, jnp.float32))
-    for h in range(2):
-        first[h][1].wait_recv()
-        third[h][0].start()
-    for h in range(2):
-        second[h][1].wait_recv()
-        third[h][1].start()
-    for h in range(2):
-        second[h][0].wait_recv()
-        first[h][2].wait_recv()
+    top = lax.fori_loop(0, n_w // 2, logits_step, jnp.full((rows, LANES), -jnp.inf, jnp.float32))
+    mi_copy.start()
+    pass_x(PIECES - 1)
+    pass_y(PIECES - 2)
+    top = lax.fori_loop(n_w // 2, n_w, logits_step, top)
+    pass_y(PIECES - 1)
+    for j in range(PIECES):
+        second[j][0].wait_recv()
+        first[j][2].wait_recv()
     fourth[1].start()
     fourth[2].start()
     row_top = jnp.broadcast_to(jnp.max(top, axis=1, keepdims=True), (rows, LANES))
-    labels = y_ref[...]
+    labels_f = spread_row(y_ref[...].astype(jnp.float32))
+    labels = labels_f.astype(jnp.int32)
     zero = jnp.zeros((rows, LANES), jnp.float32)
 
     def stat_step(k, carry):
@@ -194,7 +216,7 @@
 
     total, target, valid_sum = lax.fori_loop(0, n_w, stat_step, (zero, zero, zero))
     lane = lax.broadcasted_iota(jnp.int32, (rows, LANES), 1)
-    packed = jnp.where(lane == 0, row_top, jnp.where(lane == 1, jnp.sum(total, axis=1, keepdims=True), jnp.where(lane == 2, jnp.sum(target, axis=1, keepdims=True), jnp.sum(valid_sum, axis=1, keepdims=True))))
+    packed = jnp.where(lane == 0, row_top, jnp.where(lane == 1, jnp.sum(total, axis=1, keepdims=True), jnp.where(lane == 2, jnp.sum(target, axis=1, keepdims=True), jnp.where(lane == 3, jnp.sum(valid_sum, axis=1, keepdims=True), labels_f))))
     stat_send[...] = packed.T[:8]
     stat_recv[me] = stat_send[...]
 
@@ -203,6 +225,8 @@
 
     stat_copies = [stat_copy(k) for k in range(1, 16)]
     for c in stat_copies:
+        c.start()
+    for c in flushes[:3]:
         c.start()
     for c in stat_copies:
         c.wait()
@@ -217,8 +241,9 @@
         lse_q = lse_of(q)
         lse_ref[q:q + 1, :] = lse_q
         a, b = stat_recv[q], stat_recv[8 + q]
+        yf_ref[q:q + 1, :] = a[4:5]
         loss = loss + lse_q - (1.0 - SMOOTH) * (a[2:3] + b[2:3]) - (SMOOTH / VALID_CLASSES) * (a[3:4] + b[3:4])
-    loss_ref[...] = jnp.broadcast_to(loss, loss_ref.shape)
+    loss_ref[...] = jnp.broadcast_to(jnp.sum(loss, axis=1, keepdims=True) * (1.0 / rows_total), loss_ref.shape)
     lse_own = spread_row(lse_of(d))
     dpool_ref[...] = jnp.zeros_like(dpool_ref)
 
@@ -231,10 +256,14 @@
         return carry
 
     lax.fori_loop(0, n_w, dpool_step, 0)
-    for h in range(2):
-        third[h][0].wait_recv()
-        third[h][1].wait_recv()
+    for j in range(PIECES):
+        third[j][0].wait_recv()
+        third[j][1].wait_recv()
     fourth[3].start()
+    for c in fourth[:3]:
+        c.wait_recv()
+    for c in flushes[3:7]:
+        c.start()
     dpool = dpool_ref[...]
     part[0:1, :] = jnp.sum(dpool * pool[pl.ds(d * rows, rows), :], axis=0, keepdims=True)
     part[1:2, :] = jnp.sum(dpool, axis=0, keepdims=True)
@@ -251,16 +280,17 @@
     mine = lane_t // half == t
     mean_ref[...] = jnp.where(mine, mean_ref[...], mi_recv[0])
     inv_ref[...] = jnp.where(mine, inv_ref[...], mi_recv[1])
-    for c in fourth:
-        c.wait_recv()
-    flush = pltpu.make_async_copy(pool, pool_out, out_sem)
-    flush.start()
+    fourth[3].wait_recv()
+    flushes[7].start()
     for c in part_copies:
         c.wait()
-    dgb_ref[...] = jnp.sum(part_all[...], axis=0)
-    for c in first[0] + first[1] + second[0] + second[1] + third[0] + third[1] + fourth:
+    parts = jnp.sum(part_all[...], axis=0)
+    dgamma_ref[...] = parts[0:1].reshape(width)
+    dbeta_ref[...] = parts[1:2].reshape(width)
+    for c in sum(first + second + third, []) + fourth:
         c.wait_send()
-    flush.wait()
+    for c in flushes:
+        c.wait()
 
 
 def front_call(feats, w_head, b_head, ln_gamma, ln_beta, labels, n_data):
@@ -275,7 +305,7 @@
         front_kernel,
         name="front",
         in_specs=[anym, anym, vmem, vmem, vmem, vmem],
-        out_specs=[anym, vmem, vmem, vmem, vmem, vmem, vmem],
+        out_specs=[anym] + [vmem] * 8,
         out_shape=[
             jax.ShapeDtypeStruct((rows * n_data, width), f32),
             stat,
@@ -283,7 +313,9 @@
             jax.ShapeDtypeStruct((rows, width), f32),
             jax.ShapeDtypeStruct((8, LANES), f32),
             jax.ShapeDtypeStruct((8, LANES), f32),
-            jax.ShapeDtypeStruct((2, width), f32),
+            jax.ShapeDtypeStruct((8, LANES), f32),
+            jax.ShapeDtypeStruct((width,), f32),
+            jax.ShapeDtypeStruct((width,), f32),
         ],
         scratch_shapes=[
             pltpu.VMEM((SLOTS, GROUP, tokens, width), jnp.bfloat16),
@@ -299,16 +331,16 @@
             pltpu.VMEM((2, tokens, LANES), f32),
             pltpu.SemaphoreType.DMA((SLOTS,)),
             pltpu.SemaphoreType.DMA((n_w,)),
-            pltpu.SemaphoreType.DMA((19,)),
-            pltpu.SemaphoreType.DMA((19,)),
+            pltpu.SemaphoreType.DMA((33,)),
+            pltpu.SemaphoreType.DMA((33,)),
             pltpu.SemaphoreType.DMA((15,)),
             pltpu.SemaphoreType.DMA((15,)),
             pltpu.SemaphoreType.DMA((15,)),
             pltpu.SemaphoreType.DMA((15,)),
-            pltpu.SemaphoreType.DMA,
+            pltpu.SemaphoreType.DMA((8,)),
         ],
         compiler_params=pltpu.CompilerParams(collective_id=0, has_side_effects=True, vmem_limit_bytes=63 * 2**20),
-    )(feats, w_head, b_head.reshape(n_w, 1, WCOLS), ln_gamma[None, :], ln_beta[None, :], jnp.broadcast_to(labels[:, None], (rows, LANES)))
+    )(feats, w_head, b_head.reshape(n_w, 1, WCOLS), ln_gamma, ln_beta, labels[None, :])
 
 
 def head_kernel(shard_cols, pool_ref, gamma_ref, beta_ref, lse_ref, y_ref, w_ref, b_ref, dw_ref, db_ref, p_ref, pt_ref, lse_b, y_b, dl_ref):
@@ -319,10 +351,10 @@
     def _():
         def fill(r, carry):
             sl = pl.ds(r * LANES, LANES)
-            p = pool_ref[sl, :] * gamma_ref[...] + beta_ref[...]
+            p = pool_ref[sl, :] * gamma_ref[...].reshape(1, width) + beta_ref[...].reshape(1, width)
             p_ref[sl, :] = p.astype(jnp.bfloat16)
             lse_b[sl, :] = spread_row(lse_ref[pl.ds(r, 1), :])
-            y_b[sl, :] = spread_row(y_ref[pl.ds(r, 1), :])
+            y_b[sl, :] = spread_row(y_ref[pl.ds(r, 1), :]).astype(jnp.int32)
             return carry
 
         lax.fori_loop(0, rows // LANES, fill, 0)
@@ -330,7 +362,9 @@
             pt_ref[:, r * LANES:(r + 1) * LANES] = p_ref[r * LANES:(r + 1) * LANES, :].T
 
     base = lax.axis_index("tp") * shard_cols + block * COLS
-    for s in range(COLS // SUB):
+    n_sub = COLS // SUB
+
+    def first_half(s):
         sub = pl.ds(s * SUB, SUB)
         logits = jnp.dot(p_ref[...], w_ref[:, sub], preferred_element_type=jnp.float32)
         col = base + s * SUB + lax.broadcasted_iota(jnp.int32, (1, SUB), 1)
@@ -342,8 +376,15 @@
         dlogit = (soft - jnp.where(repeat_lanes(y_b[...], SUB) == col, target, smooth)) * (1.0 / rows)
         db_ref[:, sub] = jnp.sum(dlogit, axis=0, keepdims=True)
         dl_ref[s] = dlogit.astype(jnp.bfloat16)
-    for s in range(COLS // SUB):
+
+    def second_half(s):
         dw_ref[:, pl.ds(s * SUB, SUB)] = jnp.dot(pt_ref[...], dl_ref[s], preferred_element_type=jnp.float32)
+
+    first_half(0)
+    for s in range(1, n_sub):
+        first_half(s)
+        second_half(s - 1)
+    second_half(n_sub - 1)
 
 
 def resident(shape):
@@ -360,8 +401,8 @@
         grid=(steps,),
         in_specs=[
             resident((rows, width)),
-            resident((1, width)),
-            resident((1, width)),
+            resident((width,)),
+            resident((width,)),
             resident((8, LANES)),
             resident((8, LANES)),
             pl.BlockSpec((width, COLS), lambda g: (0, g)),
@@ -376,32 +417,33 @@
             pltpu.VMEM((rows, LANES), jnp.int32),
             pltpu.VMEM((COLS // SUB, rows, SUB), jnp.bfloat16),
         ],
-        compiler_params=pltpu.CompilerParams(vmem_limit_bytes=48 * 2**20),
+        compiler_params=pltpu.CompilerParams(vmem_limit_bytes=56 * 2**20),
         cost_estimate=pl.CostEstimate(flops=4 * rows * width * shard_cols, bytes_accessed=6 * width * shard_cols, transcendentals=rows * shard_cols),
-    )(pool, ln_gamma[None, :], ln_beta[None, :], lse_all, y_all, w_head, b_head[None, :])
+    )(pool, ln_gamma, ln_beta, lse_all, y_all, w_head, b_head[None, :])
     return dw, db[0]
 
 
-def feat_kernel(x_ref, mean_ref, inv_ref, own_ref, other_ref, gamma_ref, df_ref):
+def feat_kernel(x_ref, mean_ref, inv_ref, own_ref, other_ref, gamma_ref, df_ref, mean_t, inv_t):
     imgs, tokens, width = x_ref.shape
     chunks = tokens // ROW_TILE
     turn = (LANES - pl.program_id(0) * IMGS) % LANES
-    u_all = (own_ref[...] + other_ref[...]) * gamma_ref[...] * (1.0 / tokens)
-    us_all = jnp.sum(u_all, axis=1, keepdims=True)
+    mean_t[...] = pltpu.roll(mean_ref[...], turn, axis=1)
+    inv_t[...] = pltpu.roll(inv_ref[...], turn, axis=1)
+    u_all = (own_ref[...] + other_ref[...]) * gamma_ref[...].reshape(1, width) * (1.0 / tokens)
+    us_all = jnp.sum(u_all, axis=1, keepdims=True) * (1.0 / width)
     for i in range(imgs):
         u = u_all[i:i + 1, :]
-        us = us_all[i:i + 1, :]
-        um = us * (1.0 / width)
+        um = jnp.broadcast_to(us_all[i:i + 1, :], (ROW_TILE, LANES))
         for c in range(chunks):
             rows = pl.ds(c * ROW_TILE, ROW_TILE)
-            mean = pltpu.roll(mean_ref[rows, :], turn, axis=1)[:, i:i + 1]
-            inv = pltpu.roll(inv_ref[rows, :], turn, axis=1)[:, i:i + 1]
+            mean = jnp.broadcast_to(mean_t[rows, i:i + 1], (ROW_TILE, LANES))
+            inv = jnp.broadcast_to(inv_t[rows, i:i + 1], (ROW_TILE, LANES))
             x = x_ref[i, rows, :].astype(jnp.float32)
-            proj = (jnp.sum(x * u, axis=1, keepdims=True) - mean * us) * (inv * (1.0 / width))
-            slope = -(inv * inv * proj)
+            dots = jnp.broadcast_to(jnp.sum(x * u, axis=1, keepdims=True), (ROW_TILE, LANES))
+            slope = -(inv * inv * inv) * (dots * (1.0 / width) - mean * um)
             offset = -(inv * um) - slope * mean
             x = x_ref[i, rows, :].astype(jnp.float32)
-            df_ref[i, rows, :] = (x * slope + (u * inv + offset)).astype(jnp.bfloat16)
+            df_ref[i, rows, :] = (x * repeat_lanes(slope, width) + (u * repeat_lanes(inv, width) + repeat_lanes(offset, width))).astype(jnp.bfloat16)
 
 
 def feat_call(feats, mean, inv, own, other, ln_gamma):
@@ -411,24 +453,23 @@
         feat_kernel,
         name="feat",
         grid=(rows // IMGS,),
-        in_specs=[img((IMGS, tokens, width)), resident((tokens, LANES)), resident((tokens, LANES)), img((IMGS, width)), img((IMGS, width)), resident((1, width))],
+        in_specs=[img((IMGS, tokens, width)), resident((tokens, LANES)), resident((tokens, LANES)), img((IMGS, width)), img((IMGS, width)), resident((width,))],
         out_specs=img((IMGS, tokens, width)),
+        scratch_shapes=[pltpu.VMEM((tokens, LANES), jnp.float32)] * 2,
         out_shape=jax.ShapeDtypeStruct(feats.shape, jnp.bfloat16),
         compiler_params=pltpu.CompilerParams(vmem_limit_bytes=48 * 2**20),
         cost_estimate=pl.CostEstimate(flops=10 * rows * tokens * width, bytes_accessed=4 * rows * tokens * width, transcendentals=0),
-    )(feats, mean, inv, own, other, ln_gamma[None, :])
+    )(feats, mean, inv, own, other, ln_gamma)
 
 
 def solution(mesh):
     n_data = mesh.shape["dp"]
 
     def local_head(feats, ln_gamma, ln_beta, w_head, b_head, labels):
-        rows = feats.shape[0]
-        y_all = lax.all_gather(labels, "dp", axis=0, tiled=False)
-        pool, mean, inv, dpool, lse_all, loss, dgb = front_call(feats, w_head, b_head, ln_gamma, ln_beta, labels, n_data)
+        pool, mean, inv, dpool, lse_all, y_all, loss, dgamma, dbeta = front_call(feats, w_head, b_head, ln_gamma, ln_beta, labels, n_data)
         dpool_other = lax.ppermute(dpool, "tp", [(0, 1), (1, 0)])
         dw, db = head_call(pool, ln_gamma, ln_beta, lse_all, y_all, w_head, b_head)
         df = feat_call(feats, mean, inv, dpool, dpool_other, ln_gamma)
-        return jnp.sum(loss[0]) / (rows * n_data), df, dw, db, dgb[0], dgb[1]
+        return loss[0, 0], df, dw, db, dgamma, dbeta
 
     return jax.shard_map(local_head, mesh=mesh, in_specs=(P("dp", None, None), P(), P(), P(None, "tp"), P("tp"), P("dp")), out_specs=(P(), P("dp", None, None), P(None, "tp"), P("tp"), P(), P()), check_vma=False)

time: 243 us -> 205 us (0.84)
  Pallas kernels: 225 us -> 200 us
  blocking collectives: 8.66 us -> 0 us
  local copies, waits for them, and re-layouts: 5.34 us -> 2.41 us
    pallas_call x1, Pallas kernels: 63.4 us -> 49 us  [feat_call(): pl.pallas_call(feat_kernel, name='feat', grid=(rows // IMGS,), in_specs=[...]
    all_gather x1 -> x0, blocking collectives: 8.66 us -> none  [local_head(): y_all = lax.all_gather(labels, 'dp', axis=0, tiled=False)]
    pallas_call x1, Pallas kernels: 71.5 us -> 66.5 us  [front_call(): pl.pallas_call(front_kernel, name='front', in_specs=[anym, anym, vmem, vm...]
    pallas_call x1, Pallas kernels: 89.6 us -> 84.9 us  [head_call(): pl.pallas_call(functools.partial(head_kernel, shard_cols), name='head', g...]
    broadcast_in_dim x3 -> x0, local copies, waits for them, and re-layouts: 4 us -> none  [the longest x1 1.38 us: front_call(): jnp.broadcast_to(labels[:, None], (rows, LANES))]
  transfers between devices with their start and end apart: 1 -> 1, of which waited for: 0 -> 0; matrix products, arithmetic and copies ran while one was open for 1% -> 1% of each run, Pallas kernels for 37% -> 42%
where the time goes in v3:
time: 205 us; the launch traced here: 204 us
  Pallas kernels  200 us (98%)
  local copies, waits for them, and re-layouts  2.41 us (1%)
    pallas_call x1, Pallas kernels, head_call(): pl.pallas_call(functools.partial(head_kernel, shard_cols), name='head', g...  84.9 us
    pallas_call x1, Pallas kernels, front_call(): pl.pallas_call(front_kernel, name='front', in_specs=[anym, anym, vmem, vm...  66.5 us
    pallas_call x1, Pallas kernels, feat_call(): pl.pallas_call(feat_kernel, name='feat', grid=(rows // IMGS,), in_specs=[...  49 us
  transfers between devices with their start and end apart: 1, of which 0 were waited for; matrix products, arithmetic and copies ran while one was open for 1% of the time, Pallas kernels for 42%

profile of v3, /device:TPU:0, one launch (start us, length us, event | category | flops | bytes accessed | tf_op | source)
XLA Modules:
  0.0 204.4 jit_solution(8542482210272263367)
XLA Ops:
  0.6 66.5 %front.1 = (f32[1024,1536]{1,0:T(8,128)}, f32[144,128]{1,0:T(8,128)}, f32[144,128]{1,0:T(8,128)}, f32[128,1536]{1,0:T(8,128)}, f32[8,128]{1,0:T(8,128)}, /*index...) custom-call(bf16[128,144,1536]{2,1,0:T(8,128)(2,1)} %x_ref.1, bf16[1536,11264]{1,0:T(8,128)(2,1)} %w_ref.1, ...), custom_call_target="tpu_custom_call" | custom-call | tf_op jit(solution)/shard_map/front/pallas_call | solution.py:304
  67.1 0.9 collective-permute-start
  68.0 0.0 copy-start
  68.0 0.0 copy-start.1
  68.0 0.0 copy-start.2
  68.0 0.0 copy-start.3
  68.0 84.9 %head.1 = (f32[1536,11264]{1,0:T(8,128)}, f32[1,11264]{1,0:T(1,128)}) custom-call(f32[1024,1536]{1,0:T(8,128)} %get-tuple-element.21.pool_ref, f32[1536]{0:T(1024)} %gamma_ref.5, f32[1536]{0:T(1024)} %beta_ref.3, f32[8,128]{1,0:T(8,128)} %get-tuple-element.22.lse_ref, f32[8,128]{1,0:T(8,128)} %get-tuple-element.23.y_ref, bf16[1536,11264]{1,0:T(8,128)(2,1)} %w_ref.1, ...), custom_call_target="tpu_custom_call" | custom-call | flops 70866960384 | bytes 103809024 | tf_op jit(solution)/shard_map/head/pallas_call | solution.py:398
  153.0 1.2 slice.3
  154.2 0.0 collective-permute-done.other_ref
  154.2 0.0 copy-done
  154.2 0.0 copy-done.1
  154.2 0.0 copy-done.2
  154.2 0.0 copy-done.3
  154.2 0.0 copy-start.5
  154.2 0.0 copy-start.4
  154.2 49.0 %feat.1 = bf16[128,144,1536]{2,1,0:T(8,128)(2,1)} custom-call(bf16[128,144,1536]{2,1,0:T(8,128)(2,1)} %x_ref.1, f32[144,128]{1,0:T(8,128)S(1)} %copy-done.1, f32[144,128]{1,0:T(8,128)S(1)} %copy-done.2, f32[128,1536]{1,0:T(8,128)S(1)} %copy-done, f32[128,1536]{1,0:T(8,128)S(1)} %collective-permute-done.other_ref, f32[1536]{0:T(1024)S(1)} %copy-done.3), custom_call_target="tpu_custom_call" | custom-call | flops 283115520 | bytes 113246208 | tf_op jit(solution)/shard_map/feat/pallas_call | solution.py:452
  203.2 0.0 copy-done.5
  203.2 0.6 copy.14
  203.8 0.0 copy-done.4
  203.8 0.6 copy.15
Async XLA Ops:
  67.1 87.0 %collective-permute-start = (f32[128,1536]{1,0:T(8,128)}, f32[128,1536]{1,0:T(8,128)S(1)}, u32[]{:S(2)}, u32[]{:S(2)}) collective-permute-start(f32[128,1536]{1,0:T(8,128)} %get-tuple-element.20.own_ref), channel_id=1, source_target_pairs={{0,8},{8,0},{1,9},{9,1},{2,10},{10,2},{3,11},{11,3},{4,12},{12,4},... | collective-permute-start | bytes 2359304 | tf_op jit(solution)/shard_map/ppermute | solution.py:470
  68.0 86.2 %copy-start = (f32[128,1536]{1,0:T(8,128)S(1)}, f32[128,1536]{1,0:T(8,128)}, u32[]{:S(2)}) copy-start(f32[128,1536]{1,0:T(8,128)} %get-tuple-element.20.own_ref) | copy-start | bytes 2359300
  68.0 86.2 %copy-start.1 = (f32[144,128]{1,0:T(8,128)S(1)}, f32[144,128]{1,0:T(8,128)}, u32[]{:S(2)}) copy-start(f32[144,128]{1,0:T(8,128)} %get-tuple-element.18.mean_ref) | copy-start | bytes 221188
  68.0 86.2 %copy-start.2 = (f32[144,128]{1,0:T(8,128)S(1)}, f32[144,128]{1,0:T(8,128)}, u32[]{:S(2)}) copy-start(f32[144,128]{1,0:T(8,128)} %get-tuple-element.19.inv_ref) | copy-start | bytes 221188
  68.0 86.2 %copy-start.3 = (f32[1536]{0:T(1024)S(1)}, f32[1536]{0:T(1024)}, u32[]{:S(2)}) copy-start(f32[1536]{0:T(1024)} %gamma_ref.5) | copy-start | bytes 18436
  154.2 49.0 %copy-start.5 = (f32[1536]{0:T(1024)S(1)}, f32[1536]{0:T(1024)}, u32[]{:S(2)}) copy-start(f32[1536]{0:T(1024)} %get-tuple-element.38) | copy-start | bytes 18436
  154.2 49.6 %copy-start.4 = (f32[1536]{0:T(1024)S(1)}, f32[1536]{0:T(1024)}, u32[]{:S(2)}) copy-start(f32[1536]{0:T(1024)} %get-tuple-element.39) | copy-start | bytes 18436

commit v4 on v3

--- a/solution.py
+++ b/solution.py
@@ -12,7 +12,7 @@
 LN_EPS = 1e-5
 SMOOTH = 0.1
 LANES = 128
-COLS = 1024
+COLS = 512
 SUB = 256
 IMGS = 8
 ROW_TILE = 16
@@ -20,6 +20,7 @@
 WCOLS = 1024
 SLOTS = 3
 PIECES = 4
+PARTS = 2
 
 
 def repeat_lanes(tile, width):
@@ -60,7 +61,7 @@
 
 
 def front_kernel(x_hbm, w_hbm, b_ref, gamma_ref, beta_ref, y_ref,
-                 pool_out, mean_ref, inv_ref, dpool_ref, lse_ref, yf_ref, loss_ref, dgamma_ref, dbeta_ref,
+                 pool_out, mean_ref, inv_ref, dpool_ref, lse_ref, yf_ref, small_ref,
                  x_buf, w_buf, pool, logits, p16, stat_send, stat_recv, part, part_all, mi_send, mi_recv,
                  x_sem, w_sem, send_sem, recv_sem, st_send_sem, st_recv_sem, dg_send_sem, dg_recv_sem, out_sem):
     rows, tokens, width = x_hbm.shape
@@ -243,7 +244,8 @@
         a, b = stat_recv[q], stat_recv[8 + q]
         yf_ref[q:q + 1, :] = a[4:5]
         loss = loss + lse_q - (1.0 - SMOOTH) * (a[2:3] + b[2:3]) - (SMOOTH / VALID_CLASSES) * (a[3:4] + b[3:4])
-    loss_ref[...] = jnp.broadcast_to(jnp.sum(loss, axis=1, keepdims=True) * (1.0 / rows_total), loss_ref.shape)
+    small_ref[2:3, :] = jnp.broadcast_to(jnp.sum(loss, axis=1, keepdims=True) * (1.0 / rows_total), (1, width))
+    small_ref[3:8, :] = jnp.zeros((5, width), jnp.float32)
     lse_own = spread_row(lse_of(d))
     dpool_ref[...] = jnp.zeros_like(dpool_ref)
 
@@ -284,9 +286,7 @@
     flushes[7].start()
     for c in part_copies:
         c.wait()
-    parts = jnp.sum(part_all[...], axis=0)
-    dgamma_ref[...] = parts[0:1].reshape(width)
-    dbeta_ref[...] = parts[1:2].reshape(width)
+    small_ref[0:2, :] = jnp.sum(part_all[...], axis=0)
     for c in sum(first + second + third, []) + fourth:
         c.wait_send()
     for c in flushes:
@@ -305,7 +305,7 @@
         front_kernel,
         name="front",
         in_specs=[anym, anym, vmem, vmem, vmem, vmem],
-        out_specs=[anym] + [vmem] * 8,
+        out_specs=[anym] + [vmem] * 6,
         out_shape=[
             jax.ShapeDtypeStruct((rows * n_data, width), f32),
             stat,
@@ -313,9 +313,7 @@
             jax.ShapeDtypeStruct((rows, width), f32),
             jax.ShapeDtypeStruct((8, LANES), f32),
             jax.ShapeDtypeStruct((8, LANES), f32),
-            jax.ShapeDtypeStruct((8, LANES), f32),
-            jax.ShapeDtypeStruct((width,), f32),
-            jax.ShapeDtypeStruct((width,), f32),
+            jax.ShapeDtypeStruct((8, width), f32),
         ],
         scratch_shapes=[
             pltpu.VMEM((SLOTS, GROUP, tokens, width), jnp.bfloat16),
@@ -343,17 +341,16 @@
     )(feats, w_head, b_head.reshape(n_w, 1, WCOLS), ln_gamma, ln_beta, labels[None, :])
 
 
-def head_kernel(shard_cols, pool_ref, gamma_ref, beta_ref, lse_ref, y_ref, w_ref, b_ref, dw_ref, db_ref, p_ref, pt_ref, lse_b, y_b, dl_ref):
-    block = pl.program_id(0)
+def fill_rows(pool_ref, gamma_ref, beta_ref, lse_ref, y_ref, p_ref, pt_ref, lse_b, y_b):
     rows, width = p_ref.shape
 
-    @pl.when(block == 0)
+    @pl.when(pl.program_id(0) == 0)
     def _():
         def fill(r, carry):
             sl = pl.ds(r * LANES, LANES)
             p = pool_ref[sl, :] * gamma_ref[...].reshape(1, width) + beta_ref[...].reshape(1, width)
             p_ref[sl, :] = p.astype(jnp.bfloat16)
-            lse_b[sl, :] = spread_row(lse_ref[pl.ds(r, 1), :])
+            lse_b[sl, :] = spread_row(lse_ref[pl.ds(r, 1), :] + math.log(rows))
             y_b[sl, :] = spread_row(y_ref[pl.ds(r, 1), :]).astype(jnp.int32)
             return carry
 
@@ -361,115 +358,155 @@
         for r in range(rows // LANES):
             pt_ref[:, r * LANES:(r + 1) * LANES] = p_ref[r * LANES:(r + 1) * LANES, :].T
 
-    base = lax.axis_index("tp") * shard_cols + block * COLS
-    n_sub = COLS // SUB
-
-    def first_half(s):
+
+def head_pieces(base, p_ref, pt_ref, lse_b, y_b, w_ref, b_ref, dw_ref, db_ref, dl_ref, parts):
+    rows, width = p_ref.shape
+
+    def first_half(s, m):
         sub = pl.ds(s * SUB, SUB)
-        logits = jnp.dot(p_ref[...], w_ref[:, sub], preferred_element_type=jnp.float32)
+        part = pl.ds(m * (rows // parts), rows // parts)
+        logits = jnp.dot(p_ref[part, :], w_ref[:, sub], preferred_element_type=jnp.float32)
         col = base + s * SUB + lax.broadcasted_iota(jnp.int32, (1, SUB), 1)
         valid = col < VALID_CLASSES
-        smooth = jnp.where(valid, SMOOTH / VALID_CLASSES, 0.0)
-        target = smooth + (1.0 - SMOOTH)
+        smooth = jnp.where(valid, SMOOTH / VALID_CLASSES / rows, 0.0)
+        target = smooth + (1.0 - SMOOTH) / rows
         bias = jnp.where(valid, b_ref[:, sub], -jnp.inf)
-        soft = jnp.exp((logits + bias) - repeat_lanes(lse_b[...], SUB))
-        dlogit = (soft - jnp.where(repeat_lanes(y_b[...], SUB) == col, target, smooth)) * (1.0 / rows)
-        db_ref[:, sub] = jnp.sum(dlogit, axis=0, keepdims=True)
-        dl_ref[s] = dlogit.astype(jnp.bfloat16)
-
-    def second_half(s):
-        dw_ref[:, pl.ds(s * SUB, SUB)] = jnp.dot(pt_ref[...], dl_ref[s], preferred_element_type=jnp.float32)
-
-    first_half(0)
+        soft = jnp.exp((logits + bias) - repeat_lanes(lse_b[part, :], SUB))
+        dlogit = soft - jnp.where(repeat_lanes(y_b[part, :], SUB) == col, target, smooth)
+        db = jnp.sum(dlogit, axis=0, keepdims=True)
+        db_ref[:, sub] = db if m == 0 else db_ref[:, sub] + db
+        dl_ref[s, part, :] = dlogit.astype(jnp.bfloat16)
+
+    def second_half(s, m):
+        part = pl.ds(m * (width // parts), width // parts)
+        dw_ref[part, pl.ds(s * SUB, SUB)] = jnp.dot(pt_ref[part, :], dl_ref[s], preferred_element_type=jnp.float32)
+
+    n_sub = COLS // SUB
+    order = [functools.partial(first_half, 0, m) for m in range(parts)]
     for s in range(1, n_sub):
-        first_half(s)
-        second_half(s - 1)
-    second_half(n_sub - 1)
+        order += [functools.partial(first_half, s, m) for m in range(parts)]
+        order += [functools.partial(second_half, s - 1, m) for m in range(parts)]
+    return order + [functools.partial(second_half, n_sub - 1, m) for m in range(parts)]
+
+
+def head_kernel(shard_cols, pool_ref, gamma_ref, beta_ref, lse_ref, y_ref, w_ref, b_ref, dw_ref, db_ref, p_ref, pt_ref, lse_b, y_b, dl_ref):
+    fill_rows(pool_ref, gamma_ref, beta_ref, lse_ref, y_ref, p_ref, pt_ref, lse_b, y_b)
+    base = lax.axis_index("tp") * shard_cols + pl.program_id(0) * COLS
+    for piece in head_pieces(base, p_ref, pt_ref, lse_b, y_b, w_ref, b_ref, dw_ref, db_ref, dl_ref, 1):
+        piece()
+
+
+def feat_image(i, x_ref, mean_t, inv_t, u_ref, df_ref):
+    imgs, tokens, width = x_ref.shape
+    u = u_ref[pl.ds(i, 1), :]
+    um = jnp.broadcast_to(jnp.sum(u, axis=1, keepdims=True) * (1.0 / width), (ROW_TILE, LANES))
+    for c in range(tokens // ROW_TILE):
+        rows = pl.ds(c * ROW_TILE, ROW_TILE)
+        mean = jnp.broadcast_to(mean_t[rows, i:i + 1], (ROW_TILE, LANES))
+        inv = jnp.broadcast_to(inv_t[rows, i:i + 1], (ROW_TILE, LANES))
+        x = x_ref[i, rows, :].astype(jnp.float32)
+        dots = jnp.broadcast_to(jnp.sum(x * u, axis=1, keepdims=True), (ROW_TILE, LANES))
+        slope = -(inv * inv * inv) * (dots * (1.0 / width) - mean * um)
+        offset = -(inv * um) - slope * mean
+        x = x_ref[i, rows, :].astype(jnp.float32)
+        df_ref[i, rows, :] = (x * repeat_lanes(slope, width) + (u * repeat_lanes(inv, width) + repeat_lanes(offset, width))).astype(jnp.bfloat16)
+
+
+def head_feat_kernel(shard_cols, first, pool_ref, gamma_ref, beta_ref, lse_ref, y_ref, w_ref, b_ref, x_ref, mean_ref, inv_ref, own_ref, other_ref, small_ref, dw_in, db_in,
+                     dw_ref, db_ref, df_ref, small_out, p_ref, pt_ref, lse_b, y_b, dl_ref, mean_t, inv_t, u_ref):
+    imgs, tokens, width = x_ref.shape
+    fill_rows(pool_ref, gamma_ref, beta_ref, lse_ref, y_ref, p_ref, pt_ref, lse_b, y_b)
+    small_out[...] = small_ref[...]
+    turn = (LANES - pl.program_id(0) * imgs) % LANES
+    mean_t[...] = pltpu.roll(mean_ref[...], turn, axis=1)
+    inv_t[...] = pltpu.roll(inv_ref[...], turn, axis=1)
+    u_ref[...] = (own_ref[...] + other_ref[...]) * gamma_ref[...].reshape(1, width) * (1.0 / tokens)
+    base = lax.axis_index("tp") * shard_cols + (pl.program_id(0) + first) * COLS
+    pieces = head_pieces(base, p_ref, pt_ref, lse_b, y_b, w_ref, b_ref, dw_ref, db_ref, dl_ref, PARTS)
+    for n, piece in enumerate(pieces):
+        piece()
+        for i in range(n * imgs // len(pieces), (n + 1) * imgs // len(pieces)):
+            feat_image(i, x_ref, mean_t, inv_t, u_ref, df_ref)
 
 
 def resident(shape):
     return pl.BlockSpec(shape, lambda g: (0,) * len(shape), pipeline_mode=pl.Buffered(1))
 
 
-def head_call(pool, ln_gamma, ln_beta, lse_all, y_all, w_head, b_head):
+def head_calls(pool, ln_gamma, ln_beta, lse_all, y_all, w_head, b_head, feats, mean, inv, own, make_other, small):
     rows, width = pool.shape
     shard_cols = w_head.shape[1]
-    steps = shard_cols // COLS
-    dw, db = pl.pallas_call(
-        functools.partial(head_kernel, shard_cols),
-        name="head",
-        grid=(steps,),
-        in_specs=[
+    imgs_all, tokens, _ = feats.shape
+    feat_steps = imgs_all // IMGS
+    first = shard_cols // COLS - feat_steps
+    f32 = jnp.float32
+    args = (pool, ln_gamma, ln_beta, lse_all, y_all, w_head, b_head[None, :])
+    dw_shape = jax.ShapeDtypeStruct((width, shard_cols), f32)
+    db_shape = jax.ShapeDtypeStruct((1, shard_cols), f32)
+    scratch = [
+        pltpu.VMEM((rows, width), jnp.bfloat16),
+        pltpu.VMEM((width, rows), jnp.bfloat16),
+        pltpu.VMEM((rows, LANES), f32),
+        pltpu.VMEM((rows, LANES), jnp.int32),
+        pltpu.VMEM((COLS // SUB, rows, SUB), jnp.bfloat16),
+    ]
+
+    def specs(skip):
+        return [
             resident((rows, width)),
             resident((width,)),
             resident((width,)),
             resident((8, LANES)),
             resident((8, LANES)),
-            pl.BlockSpec((width, COLS), lambda g: (0, g)),
-            pl.BlockSpec((1, COLS), lambda g: (0, g)),
-        ],
-        out_specs=[pl.BlockSpec((width, COLS), lambda g: (0, g)), pl.BlockSpec((1, COLS), lambda g: (0, g))],
-        out_shape=[jax.ShapeDtypeStruct((width, shard_cols), jnp.float32), jax.ShapeDtypeStruct((1, shard_cols), jnp.float32)],
-        scratch_shapes=[
-            pltpu.VMEM((rows, width), jnp.bfloat16),
-            pltpu.VMEM((width, rows), jnp.bfloat16),
-            pltpu.VMEM((rows, LANES), jnp.float32),
-            pltpu.VMEM((rows, LANES), jnp.int32),
-            pltpu.VMEM((COLS // SUB, rows, SUB), jnp.bfloat16),
-        ],
-        compiler_params=pltpu.CompilerParams(vmem_limit_bytes=56 * 2**20),
-        cost_estimate=pl.CostEstimate(flops=4 * rows * width * shard_cols, bytes_accessed=6 * width * shard_cols, transcendentals=rows * shard_cols),
-    )(pool, ln_gamma, ln_beta, lse_all, y_all, w_head, b_head[None, :])
-    return dw, db[0]
-
-
-def feat_kernel(x_ref, mean_ref, inv_ref, own_ref, other_ref, gamma_ref, df_ref, mean_t, inv_t):
-    imgs, tokens, width = x_ref.shape
-    chunks = tokens // ROW_TILE
-    turn = (LANES - pl.program_id(0) * IMGS) % LANES
-    mean_t[...] = pltpu.roll(mean_ref[...], turn, axis=1)
-    inv_t[...] = pltpu.roll(inv_ref[...], turn, axis=1)
-    u_all = (own_ref[...] + other_ref[...]) * gamma_ref[...].reshape(1, width) * (1.0 / tokens)
-    us_all = jnp.sum(u_all, axis=1, keepdims=True) * (1.0 / width)
-    for i in range(imgs):
-        u = u_all[i:i + 1, :]
-        um = jnp.broadcast_to(us_all[i:i + 1, :], (ROW_TILE, LANES))
-        for c in range(chunks):
-            rows = pl.ds(c * ROW_TILE, ROW_TILE)
-            mean = jnp.broadcast_to(mean_t[rows, i:i + 1], (ROW_TILE, LANES))
-            inv = jnp.broadcast_to(inv_t[rows, i:i + 1], (ROW_TILE, LANES))
-            x = x_ref[i, rows, :].astype(jnp.float32)
-            dots = jnp.broadcast_to(jnp.sum(x * u, axis=1, keepdims=True), (ROW_TILE, LANES))
-            slope = -(inv * inv * inv) * (dots * (1.0 / width) - mean * um)
-            offset = -(inv * um) - slope * mean
-            x = x_ref[i, rows, :].astype(jnp.float32)
-            df_ref[i, rows, :] = (x * repeat_lanes(slope, width) + (u * repeat_lanes(inv, width) + repeat_lanes(offset, width))).astype(jnp.bfloat16)
-
-
-def feat_call(feats, mean, inv, own, other, ln_gamma):
-    rows, tokens, width = feats.shape
+            pl.BlockSpec((width, COLS), lambda g: (0, g + skip)),
+            pl.BlockSpec((1, COLS), lambda g: (0, g + skip)),
+        ]
+
+    def outs(skip):
+        return [pl.BlockSpec((width, COLS), lambda g: (0, g + skip)), pl.BlockSpec((1, COLS), lambda g: (0, g + skip))]
+
+    def cost(n):
+        return pl.CostEstimate(flops=4 * rows * width * COLS * n, bytes_accessed=6 * width * COLS * n, transcendentals=rows * COLS * n)
+
+    params = pltpu.CompilerParams(vmem_limit_bytes=56 * 2**20)
+    dw, db = pl.pallas_call(
+        functools.partial(head_kernel, shard_cols),
+        name="head",
+        grid=(first,),
+        in_specs=specs(0),
+        out_specs=outs(0),
+        out_shape=[dw_shape, db_shape],
+        scratch_shapes=scratch,
+        compiler_params=params,
+        cost_estimate=cost(first),
+    )(*args)
+    other = make_other
     img = lambda shape: pl.BlockSpec(shape, lambda g: (g,) + (0,) * (len(shape) - 1))
-    return pl.pallas_call(
-        feat_kernel,
-        name="feat",
-        grid=(rows // IMGS,),
-        in_specs=[img((IMGS, tokens, width)), resident((tokens, LANES)), resident((tokens, LANES)), img((IMGS, width)), img((IMGS, width)), resident((width,))],
-        out_specs=img((IMGS, tokens, width)),
-        scratch_shapes=[pltpu.VMEM((tokens, LANES), jnp.float32)] * 2,
-        out_shape=jax.ShapeDtypeStruct(feats.shape, jnp.bfloat16),
-        compiler_params=pltpu.CompilerParams(vmem_limit_bytes=48 * 2**20),
-        cost_estimate=pl.CostEstimate(flops=10 * rows * tokens * width, bytes_accessed=4 * rows * tokens * width, transcendentals=0),
-    )(feats, mean, inv, own, other, ln_gamma)
+    n_in = 13
+    dw, db, df, small = pl.pallas_call(
+        functools.partial(head_feat_kernel, shard_cols, first),
+        name="head_feat",
+        grid=(feat_steps,),
+        in_specs=specs(first)
+        + [img((IMGS, tokens, width)), resident((tokens, LANES)), resident((tokens, LANES)), img((IMGS, width)), img((IMGS, width)), resident(small.shape)]
+        + [pl.BlockSpec(memory_space=pl.ANY)] * 2,
+        out_specs=outs(first) + [img((IMGS, tokens, width)), pl.BlockSpec(small.shape, lambda g: (0, 0))],
+        out_shape=[dw_shape, db_shape, jax.ShapeDtypeStruct(feats.shape, jnp.bfloat16), jax.ShapeDtypeStruct(small.shape, f32)],
+        scratch_shapes=scratch + [pltpu.VMEM((tokens, LANES), f32)] * 2 + [pltpu.VMEM((IMGS, width), f32)],
+        input_output_aliases={n_in: 0, n_in + 1: 1},
+        compiler_params=params,
+        cost_estimate=cost(feat_steps),
+    )(*args, feats, mean, inv, own, other, small, dw, db)
+    return dw, db[0], df, small
 
 
 def solution(mesh):
     n_data = mesh.shape["dp"]
 
     def local_head(feats, ln_gamma, ln_beta, w_head, b_head, labels):
-        pool, mean, inv, dpool, lse_all, y_all, loss, dgamma, dbeta = front_call(feats, w_head, b_head, ln_gamma, ln_beta, labels, n_data)
+        pool, mean, inv, dpool, lse_all, y_all, small = front_call(feats, w_head, b_head, ln_gamma, ln_beta, labels, n_data)
         dpool_other = lax.ppermute(dpool, "tp", [(0, 1), (1, 0)])
-        dw, db = head_call(pool, ln_gamma, ln_beta, lse_all, y_all, w_head, b_head)
-        df = feat_call(feats, mean, inv, dpool, dpool_other, ln_gamma)
-        return loss[0, 0], df, dw, db, dgamma, dbeta
+        dw, db, df, small = head_calls(pool, ln_gamma, ln_beta, lse_all, y_all, w_head, b_head, feats, mean, inv, dpool, dpool_other, small)
+        return small[2, 0], df, dw, db, small[0], small[1]
 
     return jax.shard_map(local_head, mesh=mesh, in_specs=(P("dp", None, None), P(), P(), P(None, "tp"), P("tp"), P("dp")), out_specs=(P(), P("dp", None, None), P(None, "tp"), P("tp"), P(), P()), check_vma=False)

time: 205 us -> 201 us (0.980)
  Pallas kernels: 200 us -> 196 us
    pallas_call x2, Pallas kernels: 134 us -> 129 us  [the longest x1 99.8 us: head_calls(): pl.pallas_call(functools.partial(head_feat_kernel, shard_cols, first), na...]
  transfers between devices with their start and end apart: 1 -> 1, of which waited for: 0 -> 0; matrix products, arithmetic and copies ran while one was open for 1% -> 0% of each run, Pallas kernels for 42% -> 15%
where the time goes in v4:
time: 201 us
  Pallas kernels  196 us (98%)
  local copies, waits for them, and re-layouts  3.57 us (2%)
    pallas_call x1, Pallas kernels, head_calls(): pl.pallas_call(functools.partial(head_feat_kernel, shard_cols, first), na...  99.8 us
    pallas_call x1, Pallas kernels, front_call(): pl.pallas_call(front_kernel, name='front', in_specs=[anym, anym, vmem, vm...  66.5 us
    pallas_call x1, Pallas kernels, head_calls(): pl.pallas_call(functools.partial(head_kernel, shard_cols), name='head', g...  29.5 us
  transfers between devices with their start and end apart: 1, of which 0 were waited for; matrix products, arithmetic and copies ran while one was open for 0% of the time, Pallas kernels for 15%

profile of v4, /device:TPU:0, one launch (start us, length us, event | category | flops | bytes accessed | tf_op | source)
XLA Modules:
  0.0 200.8 jit_solution(8212980764964003475)
XLA Ops:
  0.6 66.5 %front.1 = (f32[1024,1536]{1,0:T(8,128)}, f32[144,128]{1,0:T(8,128)}, f32[144,128]{1,0:T(8,128)}, f32[128,1536]{1,0:T(8,128)}, f32[8,128]{1,0:T(8,128)}, /*index=5*/f32[8,128]{1,0:T(8,128)}, f32[8,1536]{1,0:T(8,128)}) custom-call(bf16[128,144,1536]{2,1,0:T(8,128)(2,1)} %x_ref.1, bf16[1536,11264]{1,0:T(8,128)(2,1)} %w_ref.3, f32[11,1,1024]{2,1,0:T(1,128)} %bitcast.5, ...), custom_call_target="tpu_custom_call" | custom-call | tf_op jit(solution)/shard_map/front/pallas_call | solution.py:304
  67.1 0.9 collective-permute-start
  68.0 29.5 %head.1 = (f32[1536,11264]{1,0:T(8,128)}, f32[1,11264]{1,0:T(1,128)}) custom-call(f32[1024,1536]{1,0:T(8,128)} %get-tuple-element.19.pool_ref, f32[1536]{0:T(1024)} %gamma_ref.5, f32[1536]{0:T(1024)} %beta_ref.5, f32[8,128]{1,0:T(8,128)} %get-tuple-element.20.lse_ref, f32[8,128]{1,0:T(8,128)} %get-tuple-element.21.y_ref, bf16[1536,11264]{1,0:T(8,128)(2,1)} %w_ref.3, ...), custom_call_target="tpu_custom_call" | custom-call | flops 19327352832 | bytes 28311552 | tf_op jit(solution)/shard_map/head/pallas_call | solution.py:472
  97.5 0.0 collective-permute-done.other_ref
  97.5 0.0 copy-start
  97.5 0.9 copy-done
  98.3 99.8 %head_feat.1 = (f32[1536,11264]{1,0:T(8,128)}, f32[1,11264]{1,0:T(1,128)}, bf16[128,144,1536]{2,1,0:T(8,128)(2,1)}, f32[8,1536]{1,0:T(8,128)}) custom-call(f32[1024,1536]{1,0:T(8,128)} %get-tuple-element.19.pool_ref, f32[1536]{0:T(1024)} %gamma_ref.5, f32[1536]{0:T(1024)} %beta_ref.5, ...), custom_call_target="tpu_custom_call", output_to_operand_aliasing={{0}: (13, {}), {1}: (14, {})} | custom-call | flops 51539607552 | bytes 75497472 | tf_op jit(solution)/shard_map/head_feat/pallas_call | solution.py:486
  198.1 1.2 slice.9
  199.3 1.5 slice_reduce_fusion
Async XLA Ops:
  67.1 30.4 %collective-permute-start = (f32[128,1536]{1,0:T(8,128)}, f32[128,1536]{1,0:T(8,128)S(1)}, u32[]{:S(2)}, u32[]{:S(2)}) collective-permute-start(f32[128,1536]{1,0:T(8,128)} %get-tuple-element.24.own_ref), channel_id=1, source_target_pairs={{0,8},{8,0},{1,9},{9,1},{2,10},{10,2},{3,11},{11,3},{4,12},{12,4},... | collective-permute-start | bytes 2359304 | tf_op jit(solution)/shard_map/ppermute | solution.py:508
  97.5 0.9 copy-start
